TPU v7x, 32 devices: a whole 2x2x4 slice. The times are simulated.
32 devices in a mesh: walker: 2 (over x), owner: 4 (over y, core), replica: 4 (over z).
Axes of the slice: x: 2, y: 2, z: 4, core: 2. Of those that a mesh axis runs over, the one named last changes fastest.
Arguments:
- layer_inputs: bfloat16 [4, 61440, 832], P(None, ('walker', 'owner', 'replica')), may hold values from -6 to 6
- layer_grads: bfloat16 [4, 61440, 256], P(None, ('walker', 'owner', 'replica')), may hold values from -6 to 6
- local_energy: float32 [1024], P(('walker', 'owner', 'replica')), may hold values from -3 to 1
Outputs:
- step: float32 [4, 832, 256], replicated
All inputs are finite; a program needn't handle non-finite values.
Results may differ from a plain program's by a relative error of at most 0.003.
Values sent between devices are 32-bit elements; how exact they have to be, the bound alone decides.
No kernel may reach another device: no remote copies, remote signals or barrier semaphores. Data moves between devices by JAX's collectives and lax.ppermute only.
A program may use at most 128 MiB of HBM per device.

v0:
```python
import functools

import jax
import jax.numpy as jnp
from jax import lax
from jax.experimental import pallas as pl
from jax.experimental.pallas import tpu as pltpu
from jax.sharding import PartitionSpec as P


F32 = jnp.float32
BF16 = jnp.bfloat16
LANES = 128
DAMPING = 0.1
TOL = 5e-4
MAX_STEPS = 4000
VMEM = pl.BlockSpec(memory_space=pltpu.VMEM)
SMEM = pl.BlockSpec(memory_space=pltpu.SMEM)
BIG_VMEM = 60 * 1024 * 1024


def gram(a, b):
    return lax.dot_general(a, b, (((0,), (0,)), ((), ())), preferred_element_type=F32)


def outer(a, b):
    return lax.dot_general(a, b, (((1,), (1,)), ((), ())), preferred_element_type=F32)


def layout(width_in, width_out):
    full = width_in // LANES
    blocks = [("a", i, j) for i in range(full) for j in range(i, full)]
    out_blocks = [
        ("g", i, j) for i in range(width_out // LANES) for j in range(i, width_out // LANES)
    ]
    cut = 2 * full - 1
    first = blocks[:cut] + out_blocks
    second = blocks[cut:]
    return first, second


def half_rows(width_in, width_out):
    first, second = layout(width_in, width_out)
    tail = width_in % LANES
    strips = -(-width_in // LANES)
    rows = max(len(first) * LANES, len(second) * LANES + strips * tail)
    return -(-rows // 64) * 64


def factor_kernel(where_ref, x_ref, g_ref, keep_ref, send_ref):
    width_in = x_ref.shape[1]
    width_out = g_ref.shape[2]
    full = width_in // LANES
    tail = width_in % LANES
    rows = keep_ref.shape[1]

    def panel(o_ref, i, start):
        lo = i * LANES
        hi = min(i + 2, full) * LANES
        sums = outer(x_ref[0, lo : full * LANES, :], x_ref[0, lo:hi, :])
        at = start
        for b in range((hi - lo) // LANES):
            for j in range(b, full - i):
                o_ref[0, at : at + LANES, :] = sums[
                    j * LANES : (j + 1) * LANES, b * LANES : (b + 1) * LANES
                ]
                at += LANES
        return at

    def first_half(o_ref):
        at = panel(o_ref, 0, 0)
        sums = gram(g_ref[0], g_ref[0])
        for i in range(width_out // LANES):
            for j in range(i, width_out // LANES):
                o_ref[0, at : at + LANES, :] = sums[
                    j * LANES : (j + 1) * LANES, i * LANES : (i + 1) * LANES
                ]
                at += LANES
        if at < rows:
            o_ref[0, at:, :] = jnp.zeros((rows - at, LANES), F32)

    def second_half(o_ref):
        at = 0
        for i in range(2, full, 2):
            at = panel(o_ref, i, at)
        if tail:
            last = x_ref[0, full * LANES :, :]
            strip = outer(last, x_ref[0, : full * LANES, :])
            for j in range(full):
                o_ref[0, at : at + tail, :] = strip[:, j * LANES : (j + 1) * LANES]
                at += tail
            corner = outer(last, last)
            o_ref[0, at : at + tail, :] = jnp.zeros((tail, LANES), F32)
            o_ref[0, at : at + tail, :tail] = corner
            at += tail
        if at < rows:
            o_ref[0, at:, :] = jnp.zeros((rows - at, LANES), F32)

    @pl.when(where_ref[0] == 0)
    def _():
        first_half(keep_ref)
        second_half(send_ref)

    @pl.when(where_ref[0] == 1)
    def _():
        first_half(send_ref)
        second_half(keep_ref)


def factor_sums(where, first, layers, x, g):
    _, width_in, rows = x.shape
    width_out = g.shape[2]
    packed = half_rows(width_in, width_out)
    out = jax.ShapeDtypeStruct((layers, packed, LANES), F32)
    out_spec = pl.BlockSpec((1, packed, LANES), lambda l, s: (l, 0, 0))
    return pl.pallas_call(
        factor_kernel,
        out_shape=(out, out),
        grid_spec=pltpu.PrefetchScalarGridSpec(
            num_scalar_prefetch=1,
            grid=(layers,),
            in_specs=[
                pl.BlockSpec((1, width_in, rows), lambda l, s: ((l + first) ^ s[1], 0, 0)),
                pl.BlockSpec((1, rows, width_out), lambda l, s: ((l + first) ^ s[1], 0, 0)),
            ],
            out_specs=(out_spec, out_spec),
        ),
        compiler_params=pltpu.CompilerParams(vmem_limit_bytes=BIG_VMEM),
        cost_estimate=pl.CostEstimate(
            flops=layers * rows * width_in * width_in,
            bytes_accessed=layers * (rows * (width_in + width_out) * 2 + packed * LANES * 8),
            transcendentals=0,
        ),
        name="factor_sums",
    )(where, x, g)


def grad_kernel(core_ref, x_ref, g_ref, c_ref, keep_ref, send_ref):
    parts = [
        (g_ref[0, :, j : j + LANES].astype(F32) * c_ref[...]).astype(BF16)
        for j in range(0, g_ref.shape[2], LANES)
    ]
    sums = mm(x_ref[0], jnp.concatenate(parts, axis=1))

    @pl.when(core_ref[0] == 0)
    def _():
        keep_ref[0] = sums[:, :LANES]
        send_ref[0] = sums[:, LANES:]

    @pl.when(core_ref[0] == 1)
    def _():
        keep_ref[0] = sums[:, LANES:]
        send_ref[0] = sums[:, :LANES]


def grad_sums(where, x, g, centered):
    layers, width_in, rows = x.shape
    width_out = g.shape[2]
    out = jax.ShapeDtypeStruct((layers, width_in, LANES), F32)
    out_spec = pl.BlockSpec((1, width_in, LANES), lambda l, s: (l, 0, 0))
    return pl.pallas_call(
        grad_kernel,
        out_shape=(out, out),
        grid_spec=pltpu.PrefetchScalarGridSpec(
            num_scalar_prefetch=1,
            grid=(layers,),
            in_specs=[
                pl.BlockSpec((1, width_in, rows), lambda l, s: (l ^ s[1], 0, 0)),
                pl.BlockSpec((1, rows, width_out), lambda l, s: (l ^ s[1], 0, 0)),
                pl.BlockSpec((rows, LANES), lambda l, s: (0, 0)),
            ],
            out_specs=(out_spec, out_spec),
        ),
        compiler_params=pltpu.CompilerParams(vmem_limit_bytes=BIG_VMEM),
        cost_estimate=pl.CostEstimate(
            flops=2 * layers * rows * width_in * width_out,
            bytes_accessed=layers * (rows * (width_in + width_out) * 2 + width_in * width_out * 4),
            transcendentals=0,
        ),
        name="grad_sums",
    )(where, x, g, centered)


def split3(v):
    one = v.astype(BF16)
    rest = v - one.astype(F32)
    two = rest.astype(BF16)
    three = (rest - two.astype(F32)).astype(BF16)
    return one, two, three


def mm(a, b):
    return jnp.dot(a, b, preferred_element_type=F32)


def product(a, b):
    low = mm(a[0], b[2]) + mm(a[2], b[0]) + mm(a[1], b[1])
    return mm(a[0], b[0]) + (mm(a[0], b[1]) + mm(a[1], b[0]) + low)


def conjugate_gradients(apply, exact, b_ref, y_ref, r_ref, p_ref):
    def total(v):
        return jnp.sum(v, keepdims=True)

    def wanted(residual, size):
        return (residual - (TOL * DAMPING) ** 2 * size)[0, 0] > 0

    def body(state):
        step, residual, _ = state
        p = p_ref[...]
        q = apply(p)
        alpha = residual / total(p * q)
        y = y_ref[...] + alpha * p
        y_ref[...] = y
        r = r_ref[...] - alpha * q
        r_ref[...] = r
        fresh = total(r * r)
        p_ref[...] = r + (fresh / residual) * p
        return step + 1, fresh, wanted(fresh, total(y * y))

    def steps(start):
        r = r_ref[...]
        p_ref[...] = r
        residual = total(r * r)
        step, _, _ = lax.while_loop(
            lambda state: state[2] & (state[0] < MAX_STEPS),
            body,
            (start, residual, residual[0, 0] > 0),
        )
        return step

    y_ref[...] = jnp.zeros(y_ref.shape, F32)
    r_ref[...] = b_ref[...]
    if exact is None:
        steps(jnp.int32(0))
        return

    def cycle(state):
        step = steps(state[0])
        y = y_ref[...]
        r = b_ref[...] - exact(y)
        r_ref[...] = r
        return step, wanted(total(r * r), total(y * y))

    lax.while_loop(
        lambda state: state[1] & (state[0] < MAX_STEPS), cycle, (jnp.int32(0), jnp.bool_(True))
    )


def solve_kernel(
    all_rows,
    walkers,
    width_in,
    width_out,
    s_ref,
    own0,
    own1,
    own2,
    got0,
    got1,
    got2,
    mine_ref,
    other_ref,
    a0,
    a1,
    a2,
    g0,
    g1,
    g2,
    b_ref,
    t_ref,
    y_ref,
    r_ref,
    p_ref,
):
    full = width_in // LANES
    tail = width_in % LANES
    first, second = layout(width_in, width_out)
    terms = {"a": (a0, a1, a2), "g": (g0, g1, g2)}

    def put(kind, row, col, value):
        height, width = value.shape
        for ref, term in zip(terms[kind], split3(value)):
            ref[row : row + height, col : col + width] = term

    def place(kind, i, j, value):
        value = value * (1.0 / all_rows)
        if i == j:
            rows = lax.broadcasted_iota(jnp.int32, value.shape, 0)
            cols = lax.broadcasted_iota(jnp.int32, value.shape, 1)
            value = value + jnp.where(rows == cols, jnp.float32(DAMPING), 0.0)
        put(kind, j * LANES, i * LANES, value)
        if i != j:
            put(kind, i * LANES, j * LANES, value.T)

    def unpack(half, refs):
        rows = refs[0].shape[0]

        def read(at, height):
            return refs[at // rows][at % rows : at % rows + height, :]

        at = 0
        for kind, i, j in (first, second)[half]:
            place(kind, i, j, read(at, LANES))
            at += LANES
        if half == 1 and tail:
            edge = full * LANES
            for j in range(full):
                value = read(at, tail) * (1.0 / all_rows)
                put("a", edge, j * LANES, value)
                put("a", j * LANES, edge, jnp.concatenate([value, jnp.zeros_like(value)], 0).T[:, :tail])
                at += tail
            value = read(at, tail)[:, :tail] * (1.0 / all_rows)
            rows_at = lax.broadcasted_iota(jnp.int32, value.shape, 0)
            cols_at = lax.broadcasted_iota(jnp.int32, value.shape, 1)
            put("a", edge, edge, value + jnp.where(rows_at == cols_at, jnp.float32(DAMPING), 0.0))
        b_ref[:width_in, half * LANES : (half + 1) * LANES] = refs[2][...] * (2.0 / walkers)

    padded = a0.shape[0]
    if padded > width_in:
        for ref in terms["a"]:
            ref[width_in:, :] = jnp.zeros((padded - width_in, padded), BF16)
            ref[:, width_in:] = jnp.zeros((padded, padded - width_in), BF16)
        b_ref[width_in:, :] = jnp.zeros((padded - width_in, width_out), F32)
    core = s_ref[0]

    @pl.when(core == 0)
    def _():
        unpack(0, (own0, own1, own2))
        unpack(1, (got0, got1, got2))

    @pl.when(core == 1)
    def _():
        unpack(1, (own0, own1, own2))
        unpack(0, (got0, got1, got2))

    def near(p):
        one = p.astype(BF16)
        two = (p - one.astype(F32)).astype(BF16)
        return mm(a0[...], one) + (mm(a0[...], two) + mm(a1[...], one))

    conjugate_gradients(
        near,
        lambda p: product((a0[...], a1[...], a2[...]), split3(p)),
        b_ref,
        t_ref,
        r_ref,
        p_ref,
    )
    conjugate_gradients(
        lambda p: product(split3(p), (g0[...], g1[...], g2[...])), None, t_ref, y_ref, r_ref, p_ref
    )
    align = jnp.sum(y_ref[...] * b_ref[...])
    strip = mine_ref.shape[1] - 8

    def give(mine, other):
        for half in range(2):
            mine_ref[half, :strip, :] = mine[half * strip : (half + 1) * strip, :]
            mine_ref[half, strip:, :] = jnp.zeros((8, LANES), F32) + align
        other_ref[...] = other

    @pl.when(core == 0)
    def _():
        give(y_ref[:width_in, :LANES], y_ref[:width_in, LANES:])

    @pl.when(core == 1)
    def _():
        give(y_ref[:width_in, LANES:], y_ref[:width_in, :LANES])


def solve(scalars, own, got, all_rows, walkers, width_in, width_out):
    padded = -(-width_in // LANES) * LANES
    square = pltpu.VMEM((padded, padded), BF16)
    small = pltpu.VMEM((width_out, width_out), BF16)
    tall = pltpu.VMEM((padded, width_out), F32)
    return pl.pallas_call(
        functools.partial(solve_kernel, all_rows, walkers, width_in, width_out),
        out_shape=(
            jax.ShapeDtypeStruct((2, width_in // 2 + 8, LANES), F32),
            jax.ShapeDtypeStruct((width_in, LANES), F32),
        ),
        in_specs=[SMEM] + [VMEM] * 6,
        out_specs=(VMEM, VMEM),
        scratch_shapes=[square] * 3 + [small] * 3 + [tall] * 5,
        compiler_params=pltpu.CompilerParams(vmem_limit_bytes=BIG_VMEM),
        cost_estimate=pl.CostEstimate(
            flops=60 * width_in * width_in * width_out, bytes_accessed=4 << 20, transcendentals=0
        ),
        name="solve",
    )(scalars, *own, *got)


def finish_kernel(count, s_ref, mine, other, *refs):
    near, far, out_ref = refs[:6], refs[6:12], refs[12]
    core = s_ref[0]
    layer = s_ref[1]
    strip = mine.shape[1] - 8
    top = {0: mine[0], **{k: near[k - 1][...] for k in (1, 2, 3)}}
    low = {0: mine[1], **{k: near[k + 2][...] for k in (1, 2, 3)}}
    a = [top[k][strip : strip + 1, :] for k in range(4)]
    align = (a[0] + a[1]) + (a[2] + a[3])
    scale = jnp.sqrt(count / align)
    here = pl.ds(pl.multiple_of(core * LANES, LANES), LANES)
    there = pl.ds(pl.multiple_of((1 - core) * LANES, LANES), LANES)
    for k in range(4):
        at = layer ^ k
        out_ref[at, :strip, here] = top[k][:strip, :] * scale
        out_ref[at, strip:, here] = low[k][:strip, :] * scale
        if k:
            out_ref[at, :strip, there] = far[k - 1][:strip, :] * scale
            out_ref[at, strip:, there] = far[k + 2][:strip, :] * scale
        else:
            out_ref[at, :, there] = other[...] * scale


def finish(scalars, pieces, layers, width_in, width_out):
    return pl.pallas_call(
        functools.partial(finish_kernel, float(layers * width_in * width_out)),
        out_shape=jax.ShapeDtypeStruct((layers, width_in, width_out), F32),
        in_specs=[SMEM] + [VMEM] * len(pieces),
        out_specs=VMEM,
        compiler_params=pltpu.CompilerParams(vmem_limit_bytes=BIG_VMEM),
        name="finish",
    )(scalars, *pieces)


def swap(value, axis, bit):
    size = lax.axis_size(axis)
    return lax.ppermute(value, axis, [(i, i ^ bit) for i in range(size)])


def bit_of(axis, bit):
    return (lax.axis_index(axis) // bit) % 2


def pick(value, dim, index):
    return lax.dynamic_index_in_dim(value, index, dim, keepdims=False)


def shard_step(layer_inputs, layer_grads, local_energy):
    walk_count = lax.axis_size("walker")
    devices = walk_count * lax.axis_size("owner") * lax.axis_size("replica")
    per_walker = local_energy.shape[0]
    walkers = per_walker * devices
    layers, rows, width_in = layer_inputs.shape
    width_out = layer_grads.shape[2]
    all_rows = rows * devices

    core_bit = ("owner", 1)
    first_bit = ("walker", 1)
    second_bit = ("replica", 1)
    row_bits = [("owner", 2), ("replica", 2)]
    extra = 2
    while extra < walk_count:
        row_bits.append(("walker", extra))
        extra *= 2

    core = bit_of(*core_bit).astype(jnp.int32)
    bx = bit_of(*first_bit)
    bd = bit_of(*second_bit)
    layer = (2 * bx + bd).astype(jnp.int32)

    inputs = jnp.swapaxes(layer_inputs, 1, 2)
    scalars = jnp.stack([core, layer])
    tie = lax.optimization_barrier
    half = layers // 2

    total = jnp.broadcast_to(jnp.sum(local_energy), (8, LANES))

    def along(axes, value):
        size = 1
        for axis in axes:
            size *= lax.axis_size(axis)
        return [
            lax.ppermute(value, axes, [(i, (i + k) % size) for i in range(size)])
            for k in range(1, size)
        ]

    terms = along(("replica",), total)
    keep_far, send_far = factor_sums(scalars, half, half, inputs, layer_grads)
    keep_far, send_far, total, terms, where = tie((keep_far, send_far, total, terms, scalars))
    got_far = swap(send_far, *core_bit)
    total = total + sum(terms)
    terms = along(("owner",), total)
    where, total = tie((where, total))
    keep_own, send_own = factor_sums(where, 0, half, inputs, layer_grads)
    keep_own, send_own, total, terms, where = tie((keep_own, send_own, total, terms, where))
    got_own = swap(send_own, *core_bit)
    total = total + sum(terms)
    total = total + sum(along(("walker",), total))
    centered = local_energy[:, None] - total[:1, :] / walkers
    centered = jnp.repeat(centered, rows // per_walker, axis=0)

    bits = [first_bit, second_bit] + row_bits
    inner = (2,) * len(row_bits) + (-1, LANES)
    packed = keep_far.shape[1] // 2

    def start(parts, order):
        which = order[0]
        parts = [[v.reshape((2,) + inner) for v in pair] for pair in parts]
        if which == 0:
            return sum(parts[1]), sum(parts[0])
        if which == 1:
            return tuple(jnp.stack([sum(v[i] for v in pair) for pair in parts]) for i in (1, 0))
        mine = bit_of(*bits[which])
        return tuple(
            jnp.stack([sum(pick(v, which - 1, i) for v in pair) for pair in parts])
            for i in (1 - mine, mine)
        )

    rest = list(range(3, len(bits)))
    orders = [[0, 1, 2] + rest, [1, 0, 2] + rest, [2, 1, 0] + rest]
    out = keep_far[:, :packed] + got_far[:, :packed]
    out, where, centered = tie((out, where, centered))
    out_first = out.reshape((2,) + inner)
    keep_grads, send_grads = grad_sums(where, inputs, layer_grads, centered)
    got_grads = swap(send_grads, *core_bit)
    stay_first = (keep_own[:, :packed] + got_own[:, :packed]).reshape((2,) + inner)
    out_second, stay_second = start(
        [
            [keep_own[:, packed:], got_own[:, packed:]],
            [keep_far[:, packed:], got_far[:, packed:]],
        ],
        orders[1],
    )
    third = start(
        [[keep_grads[:half], got_grads[:half]], [keep_grads[half:], got_grads[half:]]], orders[2]
    )

    sums = []
    for colour, ((out, keep), order) in enumerate(
        zip([(out_first, stay_first), (out_second, stay_second), third], orders)
    ):
        got = swap(out, *bits[order[0]])
        left = list(range(len(bits)))
        left.remove(order[0])
        for which in order[1:]:
            dim = left.index(which)
            if which < 2:
                out = lax.index_in_dim(keep, 1, dim, False) + lax.index_in_dim(got, 1, dim, False)
                stay = lax.index_in_dim(keep, 0, dim, False) + lax.index_in_dim(got, 0, dim, False)
            else:
                mine = bit_of(*bits[which])
                out = pick(keep, dim, 1 - mine) + pick(got, dim, 1 - mine)
                stay = pick(keep, dim, mine) + pick(got, dim, mine)
            got = swap(out, *bits[which])
            keep = stay
            left.remove(which)
        piece = keep + got
        back = [w for w in order if w >= 2]
        if colour < 2:
            back = back[::-1]
        dims = []
        for which in back:
            mine = bit_of(*bits[which])
            other = swap(piece, *bits[which])
            low = jnp.where(mine == 0, piece, other)
            high = jnp.where(mine == 0, other, piece)
            piece = jnp.stack([low, high])
            dims.insert(0, which)
        rank = len(dims)
        axes = sorted(range(rank), key=lambda k: dims[k])
        piece = piece.transpose(*axes, rank, rank + 1).reshape(-1, LANES)
        sums.append(piece)

    got = [swap(piece, *core_bit) for piece in sums]
    mine, other = solve(scalars, sums, got, all_rows, walkers, width_in, width_out)

    top = {2: swap(mine[0], *first_bit), 1: swap(mine[0], *second_bit)}
    low = {1: swap(mine[1], *second_bit), 2: swap(mine[1], *first_bit)}
    top[3] = swap(top[2], *second_bit)
    low[3] = swap(low[1], *first_bit)
    near = [top[k] for k in (1, 2, 3)] + [low[k] for k in (1, 2, 3)]
    far = [swap(piece, *core_bit) for piece in near]
    return finish(scalars, (mine, other, *near, *far), layers, width_in, width_out)


def solution(mesh):
    in_specs = (
        P(None, ("walker", "owner", "replica"), None),
        P(None, ("walker", "owner", "replica"), None),
        P(("walker", "owner", "replica")),
    )
    return jax.shard_map(shard_step, mesh=mesh, in_specs=in_specs, out_specs=P(), check_vma=False)
```

profile of v0, /device:TPU:0, one launch (start us, length us, event | category | flops | bytes accessed | tf_op | source)
XLA Modules:
  0.0 231.6 jit_solution(17318330723477329274)
XLA Ops:
  0.0 1.3 reduce_sum.9
  1.3 0.6 broadcast_in_dim.7
  1.9 5.1 %collective-permute-start.2 = (f32[8,128]{1,0:T(8,128)S(1)}, f32[8,128]{1,0:T(8,128)S(1)}, u32[]{:S(2)}, u32[]{:S(2)}) collective-permute-start(f32[8,128]{1,0:T(8,128)S(1)} %broadcast_in_dim.7), channel_id=1, source_target_pairs={{0,3},{1,0},{2,1},{3,2},{4,7},{5,4},{6,5},{7,6},{8,11},{9,8},{10,9... | collective-permute-start | bytes 12296 | tf_op jit(solution)/shard_map/ppermute | solution.py:475
  7.0 1.0 collective-permute-start
  8.1 0.6 pad_add_fusion.where_ref.core_ref.s_ref
  8.7 10.0 %factor_sums.2 = (f32[2,1792,128]{2,1,0:T(8,128)}, f32[2,1792,128]{2,1,0:T(8,128)}) custom-call(s32[2]{0:T(128)} %pad_add_fusion.where_ref.core_ref.s_ref, bf16[4,832,1920]{2,1,0:T(8,128)(2,1)} %bitcast.151, bf16[4,1920,256]{2,1,0:T(8,128)(2,1)} %g_ref.5), custom_call_target="tpu_custom_call" | custom-call | flops 2658140160 | bytes 12025856 | tf_op jit(solution)/shard_map/factor_sums/pallas_call | solution.py:116
  18.7 1.6 collective-permute-start.5
  20.9 9.9 %factor_sums.3 = (f32[2,1792,128]{2,1,0:T(8,128)}, f32[2,1792,128]{2,1,0:T(8,128)}) custom-call(s32[2]{0:T(128)} %pad_add_fusion.where_ref.core_ref.s_ref, bf16[4,832,1920]{2,1,0:T(8,128)(2,1)} %bitcast.152, bf16[4,1920,256]{2,1,0:T(8,128)(2,1)} %g_ref.5), custom_call_target="tpu_custom_call" | custom-call | flops 2658140160 | bytes 12025856 | tf_op jit(solution)/shard_map/factor_sums/pallas_call | solution.py:116
  30.8 1.7 collective-permute-start.6
  32.5 1.5 collective-permute-start.8
  33.9 2.1 collective-permute-done.8
  36.2 1.0 reshape.185.c_ref
  37.3 2.2 slice_add_fusion
  39.5 1.5 collective-permute-start.9
  40.9 10.5 %grad_sums.1 = (f32[4,832,128]{2,1,0:T(8,128)}, f32[4,832,128]{2,1,0:T(8,128)}) custom-call(s32[2]{0:T(128)} %pad_add_fusion.where_ref.core_ref.s_ref, bf16[4,832,1920]{2,1,0:T(8,128)(2,1)} %bitcast.153, bf16[4,1920,256]{2,1,0:T(8,128)(2,1)} %g_ref.5, f32[1920,128]{1,0:T(8,128)} %reshape.185.c_ref), custom_call_target="tpu_custom_call" | custom-call | flops 3271557120 | bytes 20119552 | tf_op jit(solution)/shard_map/grad_sums/pallas_call | solution.py:161
  51.4 1.4 slice_add_fusion.3
  53.2 1.4 slice_add_fusion.5
  54.7 2.6 %collective-permute-start.15 = (f32[2,2,2,224,128]{4,3,2,1,0:T(8,128)S(1)}, f32[2,2,2,224,128]{4,3,2,1,0:T(8,128)S(1)}, u32[]{:S(2)}, u32[]{:S(2)}) collective-permute-start(f32[2,2,2,224,128]{4,3,2,1,0:T(8,128)S(1)} %pad_maximum_fusion), channel_id=1, source_target_pairs={{0,1},{1,0},{2,3},{3,2},{4,5},{5,4},{6,7},{7,6},{8,9},{9,8},{10,11... | collective-permute-start | bytes 2752520 | tf_op jit(solution)/shard_map/ppermute | solution.py:429
  57.3 1.3 slice_add_fusion.1
  58.7 2.2 collective-permute-done.9
  61.0 2.5 %collective-permute-start.10 = (f32[2,2,224,128]{3,2,1,0:T(8,128)S(1)}, f32[2,2,224,128]{3,2,1,0:T(8,128)S(1)}, u32[]{:S(2)}, u32[]{:S(2)}) collective-permute-start(f32[2,2,224,128]{3,2,1,0:T(8,128)S(1)} %get-tuple-element.80), channel_id=1, source_target_pairs={{0,1},{1,0},{2,3},{3,2},{4,5},{5,4},{6,7},{7,6},{8,9},{9,8},{10,11... | collective-permute-start | bytes 1376264 | tf_op jit(solution)/shard_map/ppermute | solution.py:429
  63.5 14.9 %collective-permute-done.15 = f32[2,2,2,224,128]{4,3,2,1,0:T(8,128)S(1)} collective-permute-done((f32[2,2,2,224,128]{4,3,2,1,0:T(8,128)S(1)}, f32[2,2,2,224,128]{4,3,2,1,0:T(8,128)S(1)}, u32[]{:S(2)}, u32[]{:S(2)}) %collective-permute-start.15) | collective-permute-done | bytes 917536 | tf_op jit(solution)/shard_map/ppermute | solution.py:429
  78.6 0.6 collective-permute-start.16
  79.5 0.6 collective-permute-start.22
  80.1 7.5 %collective-permute-done.10 = f32[2,2,224,128]{3,2,1,0:T(8,128)S(1)} collective-permute-done((f32[2,2,224,128]{3,2,1,0:T(8,128)S(1)}, f32[2,2,224,128]{3,2,1,0:T(8,128)S(1)}, u32[]{:S(2)}, u32[]{:S(2)}) %collective-permute-start.10) | collective-permute-done | bytes 458784 | tf_op jit(solution)/shard_map/ppermute | solution.py:429
  87.6 0.6 collective-permute-start.11
  88.2 1.6 collective-permute-done.16
  89.9 0.6 collective-permute-start.17
  90.4 16.0 %collective-permute-done.11 = f32[2,224,128]{2,1,0:T(8,128)} collective-permute-done((f32[2,224,128]{2,1,0:T(8,128)S(1)}, f32[2,224,128]{2,1,0:T(8,128)}, u32[]{:S(2)}, u32[]{:S(2)}) %collective-permute-start.11) | collective-permute-done | bytes 229408 | tf_op jit(solution)/shard_map/ppermute | solution.py:429
  106.4 0.9 fusion.13
  107.3 1.0 collective-permute-start.12
  108.3 0.6 collective-permute-done.17
  108.8 0.9 fusion.12
  109.8 1.5 collective-permute-start.18
  111.3 7.6 %collective-permute-done.12 = f32[224,128]{1,0:T(8,128)S(1)} collective-permute-done((f32[224,128]{1,0:T(8,128)S(1)}, f32[224,128]{1,0:T(8,128)S(1)}, u32[]{:S(2)}, u32[]{:S(2)}) %collective-permute-start.12) | collective-permute-done | bytes 114720 | tf_op jit(solution)/shard_map/ppermute | solution.py:429
  118.8 0.9 bitcast_add_fusion.8
  119.9 1.6 collective-permute-start.23
  121.6 0.9 bitcast_add_fusion.5
  122.5 1.4 collective-permute-start.19
  123.9 2.4 %collective-permute-done.13 = f32[224,128]{1,0:T(8,128)S(1)} collective-permute-done((f32[224,128]{1,0:T(8,128)S(1)}, f32[224,128]{1,0:T(8,128)S(1)}, u32[]{:S(2)}, u32[]{:S(2)}) %collective-permute-start.13) | collective-permute-done | bytes 114720 | tf_op jit(solution)/shard_map/ppermute | solution.py:429
  126.3 0.6 collective-permute-start.14
  126.9 4.9 %collective-permute-done.23 = f32[2,2,208,128]{3,2,1,0:T(8,128)S(1)} collective-permute-done((f32[2,2,208,128]{3,2,1,0:T(8,128)S(1)}, f32[2,2,208,128]{3,2,1,0:T(8,128)S(1)}, u32[]{:S(2)}, u32[]{:S(2)}) %collective-permute-start.23) | collective-permute-done | bytes 426016 | tf_op jit(solution)/shard_map/ppermute | solution.py:429
  131.9 1.6 collective-permute-start.24
  133.5 0.6 collective-permute-start.20
  134.1 3.7 %collective-permute-done.24 = f32[2,208,128]{2,1,0:T(8,128)S(1)} collective-permute-done((f32[2,208,128]{2,1,0:T(8,128)S(1)}, f32[2,208,128]{2,1,0:T(8,128)S(1)}, u32[]{:S(2)}, u32[]{:S(2)}) %collective-permute-start.24) | collective-permute-done | bytes 213024 | tf_op jit(solution)/shard_map/ppermute | solution.py:429
  138.2 5.7 %collective-permute-done.25 = f32[208,128]{1,0:T(8,128)S(1)} collective-permute-done((f32[208,128]{1,0:T(8,128)S(1)}, f32[208,128]{1,0:T(8,128)S(1)}, u32[]{:S(2)}, u32[]{:S(2)}) %collective-permute-start.25) | collective-permute-done | bytes 106528 | tf_op jit(solution)/shard_map/ppermute | solution.py:429
  144.5 4.1 %collective-permute-done.26 = f32[208,128]{1,0:T(8,128)S(1)} collective-permute-done((f32[208,128]{1,0:T(8,128)S(1)}, f32[208,128]{1,0:T(8,128)S(1)}, u32[]{:S(2)}, u32[]{:S(2)}) %collective-permute-start.26) | collective-permute-done | bytes 106528 | tf_op jit(solution)/shard_map/ppermute | solution.py:429
  148.9 8.1 %collective-permute-done.27 = f32[2,208,128]{2,1,0:T(8,128)S(1)} collective-permute-done((f32[2,208,128]{2,1,0:T(8,128)S(1)}, f32[2,208,128]{2,1,0:T(8,128)S(1)}, u32[]{:S(2)}, u32[]{:S(2)}) %collective-permute-start.27) | collective-permute-done | bytes 213024 | tf_op jit(solution)/shard_map/ppermute | solution.py:429
  157.2 1.7 collective-permute-done.30.got2
  159.0 0.7 copy-done.21
  159.7 45.9 %solve.1 = (f32[2,424,128]{2,1,0:T(8,128)}, f32[832,128]{1,0:T(8,128)}) custom-call(s32[2]{0:T(128)} %pad_add_fusion.where_ref.core_ref.s_ref, f32[896,128]{1,0:T(8,128)} %bitcast.165, f32[896,128]{1,0:T(8,128)} %bitcast.167, f32[832,128]{1,0:T(8,128)} %bitcast.169, f32[896,128]{1,0:T(8,128)} %copy-done.19, f32[896,128]{1,0:T(8,128)} %copy-done.20, ...), custom_call_target="tpu_custom_call" | custom-call | flops 10632560640 | bytes 4194304 | tf_op jit(solution)/shard_map/solve/pallas_call | solution.py:376
  205.7 1.1 slice_bitcast_fusion.4
  206.7 1.5 collective-permute-start.35
  208.3 0.6 collective-permute-start.32
  208.8 2.0 collective-permute-start.31
  210.8 4.2 %collective-permute-done.35.refs_4_ = f32[424,128]{1,0:T(8,128)S(1)} collective-permute-done((f32[424,128]{1,0:T(8,128)S(1)}, f32[424,128]{1,0:T(8,128)S(1)}, u32[]{:S(2)}, u32[]{:S(2)}) %collective-permute-start.35) | collective-permute-done | bytes 217120 | tf_op jit(solution)/shard_map/ppermute | solution.py:429
  215.0 1.5 collective-permute-done.34.refs_3_
  216.5 0.6 collective-permute-start.36
  217.0 2.5 %collective-permute-done.32.refs_1_ = f32[424,128]{1,0:T(8,128)S(1)} collective-permute-done((f32[424,128]{1,0:T(8,128)S(1)}, f32[424,128]{1,0:T(8,128)S(1)}, u32[]{:S(2)}, u32[]{:S(2)}) %collective-permute-start.32) | collective-permute-done | bytes 217120 | tf_op jit(solution)/shard_map/ppermute | solution.py:429
  220.6 2.9 %collective-permute-done.36.refs_5_ = f32[424,128]{1,0:T(8,128)S(1)} collective-permute-done((f32[424,128]{1,0:T(8,128)S(1)}, f32[424,128]{1,0:T(8,128)S(1)}, u32[]{:S(2)}, u32[]{:S(2)}) %collective-permute-start.36) | collective-permute-done | bytes 217120 | tf_op jit(solution)/shard_map/ppermute | solution.py:429
  223.5 1.9 collective-permute-done.33.refs_2_
  225.5 1.4 collective-permute-done.39.refs_8_
  227.0 0.6 copy-done.17
  227.6 4.0 %finish.1 = f32[4,832,256]{2,1,0:T(8,128)} custom-call(s32[2]{0:T(128)} %pad_add_fusion.where_ref.core_ref.s_ref, f32[2,424,128]{2,1,0:T(8,128)} %get-tuple-element.57.mine, f32[832,128]{1,0:T(8,128)} %get-tuple-element.58.other, f32[424,128]{1,0:T(8,128)} %copy-done.9, f32[424,128]{1,0:T(8,128)} %copy-done.8, f32[424,128]{1,0:T(8,128)} %copy-done.12, ...), custom_call_target="tpu_custom_call" | custom-call | tf_op jit(solution)/shard_map/finish/pallas_call | solution.py:417
  (116 shorter events, 4.9 us)
Async XLA Ops:
  1.9 16.7 %collective-permute-start.2 = (f32[8,128]{1,0:T(8,128)S(1)}, f32[8,128]{1,0:T(8,128)S(1)}, u32[]{:S(2)}, u32[]{:S(2)}) collective-permute-start(f32[8,128]{1,0:T(8,128)S(1)} %broadcast_in_dim.7), channel_id=1, source_target_pairs={{0,3},{1,0},{2,1},{3,2},{4,7},{5,4},{6,5},{7,6},{8,11},{9,8},{10,9... | collective-permute-start | bytes 12296 | tf_op jit(solution)/shard_map/ppermute | solution.py:475
  7.0 11.6 %collective-permute-start.1 = (f32[8,128]{1,0:T(8,128)S(1)}, f32[8,128]{1,0:T(8,128)S(1)}, u32[]{:S(2)}, u32[]{:S(2)}) collective-permute-start(f32[8,128]{1,0:T(8,128)S(1)} %broadcast_in_dim.7), channel_id=1, source_target_pairs={{0,2},{1,3},{2,0},{3,1},{4,6},{5,7},{6,4},{7,5},{8,10},{9,11},{10,... | collective-permute-start | bytes 12296 | tf_op jit(solution)/shard_map/ppermute | solution.py:475
  7.0 11.6 %collective-permute-start = (f32[8,128]{1,0:T(8,128)S(1)}, f32[8,128]{1,0:T(8,128)S(1)}, u32[]{:S(2)}, u32[]{:S(2)}) collective-permute-start(f32[8,128]{1,0:T(8,128)S(1)} %broadcast_in_dim.7), channel_id=1, source_target_pairs={{0,1},{1,2},{2,3},{3,0},{4,5},{5,6},{6,7},{7,4},{8,9},{9,10},{10,1... | collective-permute-start | bytes 12296 | tf_op jit(solution)/shard_map/ppermute | solution.py:475
  18.6 18.6 %collective-permute-start.7 = (f32[2,1792,128]{2,1,0:T(8,128)}, f32[2,1792,128]{2,1,0:T(8,128)}, u32[]{:S(2)}, u32[]{:S(2)}) collective-permute-start(f32[2,1792,128]{2,1,0:T(8,128)} %get-tuple-element.46), channel_id=1, source_target_pairs={{0,4},{4,0},{8,12},{12,8},{1,5},{5,1},{9,13},{13,9},{2,6},{6,2},{1... | collective-permute-start | bytes 5505032 | tf_op jit(solution)/shard_map/ppermute | solution.py:429
  18.7 17.3 %copy-start.18 = (f32[32]{0:T(128)S(1)}, f32[32]{0:T(128)}, u32[]{:S(2)}) copy-start(f32[32]{0:T(128)} %param.5) | copy-start | bytes 388
  18.7 12.0 %collective-permute-start.5 = (f32[8,128]{1,0:T(8,128)S(1)}, f32[8,128]{1,0:T(8,128)S(1)}, u32[]{:S(2)}, u32[]{:S(2)}) collective-permute-start(f32[8,128]{1,0:T(8,128)S(1)} %add_add_fusion.1), channel_id=1, source_target_pairs={{0,12},{4,0},{8,4},{12,8},{1,13},{5,1},{9,5},{13,9},{2,14},{6,2},{... | collective-permute-start | bytes 12296 | tf_op jit(solution)/shard_map/ppermute | solution.py:475
  20.3 10.4 %collective-permute-start.4 = (f32[8,128]{1,0:T(8,128)S(1)}, f32[8,128]{1,0:T(8,128)S(1)}, u32[]{:S(2)}, u32[]{:S(2)}) collective-permute-start(f32[8,128]{1,0:T(8,128)S(1)} %add_add_fusion.1), channel_id=1, source_target_pairs={{0,8},{4,12},{8,0},{12,4},{1,9},{5,13},{9,1},{13,5},{2,10},{6,14},... | collective-permute-start | bytes 12296 | tf_op jit(solution)/shard_map/ppermute | solution.py:475
  20.9 9.9 %collective-permute-start.3 = (f32[8,128]{1,0:T(8,128)S(1)}, f32[8,128]{1,0:T(8,128)S(1)}, u32[]{:S(2)}, u32[]{:S(2)}) collective-permute-start(f32[8,128]{1,0:T(8,128)S(1)} %add_add_fusion.1), channel_id=1, source_target_pairs={{0,4},{4,8},{8,12},{12,0},{1,5},{5,9},{9,13},{13,1},{2,6},{6,10},{... | collective-permute-start | bytes 12296 | tf_op jit(solution)/shard_map/ppermute | solution.py:475
  30.7 6.5 %copy-start = (f32[2,1792,128]{2,1,0:T(8,128)S(1)}, f32[2,1792,128]{2,1,0:T(8,128)}, u32[]{:S(2)}) copy-start(f32[2,1792,128]{2,1,0:T(8,128)} %get-tuple-element.45) | copy-start | bytes 5505028
  30.8 22.1 %collective-permute-start.6 = (f32[2,1792,128]{2,1,0:T(8,128)}, f32[2,1792,128]{2,1,0:T(8,128)}, u32[]{:S(2)}, u32[]{:S(2)}) collective-permute-start(f32[2,1792,128]{2,1,0:T(8,128)} %get-tuple-element.44), channel_id=1, source_target_pairs={{0,4},{4,0},{8,12},{12,8},{1,5},{5,1},{9,13},{13,9},{2,6},{6,2},{1... | collective-permute-start | bytes 5505032 | tf_op jit(solution)/shard_map/ppermute | solution.py:429
  32.5 3.6 %collective-permute-start.8 = (f32[8,128]{1,0:T(8,128)S(1)}, f32[8,128]{1,0:T(8,128)S(1)}, u32[]{:S(2)}, u32[]{:S(2)}) collective-permute-start(f32[8,128]{1,0:T(8,128)S(1)} %add_add_fusion), channel_id=1, source_target_pairs={{0,16},{16,0},{1,17},{17,1},{2,18},{18,2},{3,19},{19,3},{4,20},{20... | collective-permute-start | bytes 12296 | tf_op jit(solution)/shard_map/ppermute | solution.py:475
  39.5 21.4 %collective-permute-start.9 = (f32[2,2,2,224,128]{4,3,2,1,0:T(8,128)}, f32[2,2,2,224,128]{4,3,2,1,0:T(8,128)S(1)}, u32[]{:S(2)}, u32[]{:S(2)}) collective-permute-start(f32[2,2,2,224,128]{4,3,2,1,0:T(8,128)} %bitcast.5), channel_id=1, source_target_pairs={{0,16},{16,0},{1,17},{17,1},{2,18},{18,2},{3,19},{19,3},{4,20},{20... | collective-permute-start | bytes 2752520 | tf_op jit(solution)/shard_map/ppermute | solution.py:429
  51.4 1.8 copy-start.1
  51.4 27.7 %collective-permute-start.21 = (f32[4,832,128]{2,1,0:T(8,128)}, f32[4,832,128]{2,1,0:T(8,128)S(1)}, u32[]{:S(2)}, u32[]{:S(2)}) collective-permute-start(f32[4,832,128]{2,1,0:T(8,128)} %get-tuple-element.56), channel_id=1, source_target_pairs={{0,4},{4,0},{8,12},{12,8},{1,5},{5,1},{9,13},{13,9},{2,6},{6,2},{1... | collective-permute-start | bytes 5111816 | tf_op jit(solution)/shard_map/ppermute | solution.py:429
  52.8 4.4 %copy-start.2 = (f32[4,832,128]{2,1,0:T(8,128)S(1)}, f32[4,832,128]{2,1,0:T(8,128)}, u32[]{:S(2)}) copy-start(f32[4,832,128]{2,1,0:T(8,128)} %get-tuple-element.55) | copy-start | bytes 5111812
  54.7 23.8 %collective-permute-start.15 = (f32[2,2,2,224,128]{4,3,2,1,0:T(8,128)S(1)}, f32[2,2,2,224,128]{4,3,2,1,0:T(8,128)S(1)}, u32[]{:S(2)}, u32[]{:S(2)}) collective-permute-start(f32[2,2,2,224,128]{4,3,2,1,0:T(8,128)S(1)} %pad_maximum_fusion), channel_id=1, source_target_pairs={{0,1},{1,0},{2,3},{3,2},{4,5},{5,4},{6,7},{7,6},{8,9},{9,8},{10,11... | collective-permute-start | bytes 2752520 | tf_op jit(solution)/shard_map/ppermute | solution.py:429
  61.0 26.6 %collective-permute-start.10 = (f32[2,2,224,128]{3,2,1,0:T(8,128)S(1)}, f32[2,2,224,128]{3,2,1,0:T(8,128)S(1)}, u32[]{:S(2)}, u32[]{:S(2)}) collective-permute-start(f32[2,2,224,128]{3,2,1,0:T(8,128)S(1)} %get-tuple-element.80), channel_id=1, source_target_pairs={{0,1},{1,0},{2,3},{3,2},{4,5},{5,4},{6,7},{7,6},{8,9},{9,8},{10,11... | collective-permute-start | bytes 1376264 | tf_op jit(solution)/shard_map/ppermute | solution.py:429
  78.6 11.2 %collective-permute-start.16 = (f32[2,2,224,128]{3,2,1,0:T(8,128)S(1)}, f32[2,2,224,128]{3,2,1,0:T(8,128)S(1)}, u32[]{:S(2)}, u32[]{:S(2)}) collective-permute-start(f32[2,2,224,128]{3,2,1,0:T(8,128)S(1)} %get-tuple-element.76), channel_id=1, source_target_pairs={{0,16},{16,0},{1,17},{17,1},{2,18},{18,2},{3,19},{19,3},{4,20},{20... | collective-permute-start | bytes 1376264 | tf_op jit(solution)/shard_map/ppermute | solution.py:429
  79.5 40.3 %collective-permute-start.22 = (f32[2,2,2,208,128]{4,3,2,1,0:T(8,128)S(1)}, f32[2,2,2,208,128]{4,3,2,1,0:T(8,128)S(1)}, u32[]{:S(2)}, u32[]{:S(2)}) collective-permute-start(f32[2,2,2,208,128]{4,3,2,1,0:T(8,128)S(1)} %pad_maximum_fusion.1), channel_id=1, source_target_pairs={{0,8},{4,12},{8,0},{12,4},{1,9},{5,13},{9,1},{13,5},{2,10},{6,14},... | collective-permute-start | bytes 2555912 | tf_op jit(solution)/shard_map/ppermute | solution.py:429
  87.6 18.8 %collective-permute-start.11 = (f32[2,224,128]{2,1,0:T(8,128)S(1)}, f32[2,224,128]{2,1,0:T(8,128)}, u32[]{:S(2)}, u32[]{:S(2)}) collective-permute-start(f32[2,224,128]{2,1,0:T(8,128)S(1)} %get-tuple-element.78), channel_id=1, source_target_pairs={{0,8},{4,12},{8,0},{12,4},{1,9},{5,13},{9,1},{13,5},{2,10},{6,14},... | collective-permute-start | bytes 688136 | tf_op jit(solution)/shard_map/ppermute | solution.py:429
  89.9 19.0 %collective-permute-start.17 = (f32[2,224,128]{2,1,0:T(8,128)S(1)}, f32[2,224,128]{2,1,0:T(8,128)}, u32[]{:S(2)}, u32[]{:S(2)}) collective-permute-start(f32[2,224,128]{2,1,0:T(8,128)S(1)} %get-tuple-element.74), channel_id=1, source_target_pairs={{0,8},{4,12},{8,0},{12,4},{1,9},{5,13},{9,1},{13,5},{2,10},{6,14},... | collective-permute-start | bytes 688136 | tf_op jit(solution)/shard_map/ppermute | solution.py:429
  107.3 11.5 %collective-permute-start.12 = (f32[224,128]{1,0:T(8,128)S(1)}, f32[224,128]{1,0:T(8,128)S(1)}, u32[]{:S(2)}, u32[]{:S(2)}) collective-permute-start(f32[224,128]{1,0:T(8,128)S(1)} %fusion.13), channel_id=1, source_target_pairs={{0,2},{1,3},{2,0},{3,1},{4,6},{5,7},{6,4},{7,5},{8,10},{9,11},{10,... | collective-permute-start | bytes 344072 | tf_op jit(solution)/shard_map/ppermute | solution.py:429
  109.8 11.8 %collective-permute-start.18 = (f32[224,128]{1,0:T(8,128)S(1)}, f32[224,128]{1,0:T(8,128)S(1)}, u32[]{:S(2)}, u32[]{:S(2)}) collective-permute-start(f32[224,128]{1,0:T(8,128)S(1)} %fusion.12), channel_id=1, source_target_pairs={{0,2},{1,3},{2,0},{3,1},{4,6},{5,7},{6,4},{7,5},{8,10},{9,11},{10,... | collective-permute-start | bytes 344072 | tf_op jit(solution)/shard_map/ppermute | solution.py:429
  119.8 6.5 %collective-permute-start.13 = (f32[224,128]{1,0:T(8,128)S(1)}, f32[224,128]{1,0:T(8,128)S(1)}, u32[]{:S(2)}, u32[]{:S(2)}) collective-permute-start(f32[224,128]{1,0:T(8,128)S(1)} %bitcast_add_fusion.8), channel_id=1, source_target_pairs={{0,2},{1,3},{2,0},{3,1},{4,6},{5,7},{6,4},{7,5},{8,10},{9,11},{10,... | collective-permute-start | bytes 344072 | tf_op jit(solution)/shard_map/ppermute | solution.py:429
  119.9 11.9 %collective-permute-start.23 = (f32[2,2,208,128]{3,2,1,0:T(8,128)S(1)}, f32[2,2,208,128]{3,2,1,0:T(8,128)S(1)}, u32[]{:S(2)}, u32[]{:S(2)}) collective-permute-start(f32[2,2,208,128]{3,2,1,0:T(8,128)S(1)} %get-tuple-element.64), channel_id=1, source_target_pairs={{0,1},{1,0},{2,3},{3,2},{4,5},{5,4},{6,7},{7,6},{8,9},{9,8},{10,11... | collective-permute-start | bytes 1277960 | tf_op jit(solution)/shard_map/ppermute | solution.py:429
  122.5 10.9 %collective-permute-start.19 = (f32[224,128]{1,0:T(8,128)S(1)}, f32[224,128]{1,0:T(8,128)S(1)}, u32[]{:S(2)}, u32[]{:S(2)}) collective-permute-start(f32[224,128]{1,0:T(8,128)S(1)} %bitcast_add_fusion.5), channel_id=1, source_target_pairs={{0,2},{1,3},{2,0},{3,1},{4,6},{5,7},{6,4},{7,5},{8,10},{9,11},{10,... | collective-permute-start | bytes 344072 | tf_op jit(solution)/shard_map/ppermute | solution.py:429
  126.3 11.8 %collective-permute-start.14 = (f32[2,224,128]{2,1,0:T(8,128)S(1)}, f32[2,224,128]{2,1,0:T(8,128)S(1)}, u32[]{:S(2)}, u32[]{:S(2)}) collective-permute-start(f32[2,224,128]{2,1,0:T(8,128)S(1)} %pad_maximum_fusion.6), channel_id=1, source_target_pairs={{0,8},{4,12},{8,0},{12,4},{1,9},{5,13},{9,1},{13,5},{2,10},{6,14},... | collective-permute-start | bytes 688136 | tf_op jit(solution)/shard_map/ppermute | solution.py:429
  131.9 5.9 %collective-permute-start.24 = (f32[2,208,128]{2,1,0:T(8,128)S(1)}, f32[2,208,128]{2,1,0:T(8,128)S(1)}, u32[]{:S(2)}, u32[]{:S(2)}) collective-permute-start(f32[2,208,128]{2,1,0:T(8,128)S(1)} %get-tuple-element.84), channel_id=1, source_target_pairs={{0,16},{16,0},{1,17},{17,1},{2,18},{18,2},{3,19},{19,3},{4,20},{20... | collective-permute-start | bytes 638984 | tf_op jit(solution)/shard_map/ppermute | solution.py:429
  133.5 15.2 %collective-permute-start.20 = (f32[2,224,128]{2,1,0:T(8,128)S(1)}, f32[2,224,128]{2,1,0:T(8,128)S(1)}, u32[]{:S(2)}, u32[]{:S(2)}) collective-permute-start(f32[2,224,128]{2,1,0:T(8,128)S(1)} %pad_maximum_fusion.7), channel_id=1, source_target_pairs={{0,8},{4,12},{8,0},{12,4},{1,9},{5,13},{9,1},{13,5},{2,10},{6,14},... | collective-permute-start | bytes 688136 | tf_op jit(solution)/shard_map/ppermute | solution.py:429
  137.8 6.0 %collective-permute-start.25 = (f32[208,128]{1,0:T(8,128)S(1)}, f32[208,128]{1,0:T(8,128)S(1)}, u32[]{:S(2)}, u32[]{:S(2)}) collective-permute-start(f32[208,128]{1,0:T(8,128)S(1)} %fusion.14), channel_id=1, source_target_pairs={{0,2},{1,3},{2,0},{3,1},{4,6},{5,7},{6,4},{7,5},{8,10},{9,11},{10,... | collective-permute-start | bytes 319496 | tf_op jit(solution)/shard_map/ppermute | solution.py:429
  143.8 4.8 %collective-permute-start.26 = (f32[208,128]{1,0:T(8,128)S(1)}, f32[208,128]{1,0:T(8,128)S(1)}, u32[]{:S(2)}, u32[]{:S(2)}) collective-permute-start(f32[208,128]{1,0:T(8,128)S(1)} %bitcast_add_fusion.11), channel_id=1, source_target_pairs={{0,8},{4,12},{8,0},{12,4},{1,9},{5,13},{9,1},{13,5},{2,10},{6,14},... | collective-permute-start | bytes 319496 | tf_op jit(solution)/shard_map/ppermute | solution.py:429
  144.4 12.7 %copy-start.3 = (f32[2,2,224,128]{3,2,1,0:T(8,128)}, f32[2,2,224,128]{3,2,1,0:T(8,128)S(1)}, u32[]{:S(2)}) copy-start(f32[2,2,224,128]{3,2,1,0:T(8,128)S(1)} %pad_maximum_fusion.2) | copy-start | bytes 1376260
  144.4 12.8 %collective-permute-start.28 = (f32[896,128]{1,0:T(8,128)S(1)}, f32[896,128]{1,0:T(8,128)S(1)}, u32[]{:S(2)}, u32[]{:S(2)}) collective-permute-start(f32[896,128]{1,0:T(8,128)S(1)} %bitcast.164), channel_id=1, source_target_pairs={{0,4},{4,0},{8,12},{12,8},{1,5},{5,1},{9,13},{13,9},{2,6},{6,2},{1... | collective-permute-start | bytes 1376264 | tf_op jit(solution)/shard_map/ppermute | solution.py:429
  148.7 8.4 %collective-permute-start.27 = (f32[2,208,128]{2,1,0:T(8,128)S(1)}, f32[2,208,128]{2,1,0:T(8,128)S(1)}, u32[]{:S(2)}, u32[]{:S(2)}) collective-permute-start(f32[2,208,128]{2,1,0:T(8,128)S(1)} %pad_maximum_fusion.8), channel_id=1, source_target_pairs={{0,2},{1,3},{2,0},{3,1},{4,6},{5,7},{6,4},{7,5},{8,10},{9,11},{10,... | collective-permute-start | bytes 638984 | tf_op jit(solution)/shard_map/ppermute | solution.py:429
  148.8 10.1 %copy-start.4 = (f32[2,2,224,128]{3,2,1,0:T(8,128)}, f32[2,2,224,128]{3,2,1,0:T(8,128)S(1)}, u32[]{:S(2)}) copy-start(f32[2,2,224,128]{3,2,1,0:T(8,128)S(1)} %pad_maximum_fusion.3) | copy-start | bytes 1376260
  148.8 8.4 %collective-permute-start.29 = (f32[896,128]{1,0:T(8,128)S(1)}, f32[896,128]{1,0:T(8,128)S(1)}, u32[]{:S(2)}, u32[]{:S(2)}) collective-permute-start(f32[896,128]{1,0:T(8,128)S(1)} %bitcast.166), channel_id=1, source_target_pairs={{0,4},{4,0},{8,12},{12,8},{1,5},{5,1},{9,13},{13,9},{2,6},{6,2},{1... | collective-permute-start | bytes 1376264 | tf_op jit(solution)/shard_map/ppermute | solution.py:429
  157.1 1.9 copy-start.5
  157.1 1.8 collective-permute-start.30
  157.2 1.8 copy-start.19
  157.2 1.7 copy-start.20
  159.0 0.8 copy-start.21
  206.7 8.3 %collective-permute-start.35 = (f32[424,128]{1,0:T(8,128)S(1)}, f32[424,128]{1,0:T(8,128)S(1)}, u32[]{:S(2)}, u32[]{:S(2)}) collective-permute-start(f32[424,128]{1,0:T(8,128)S(1)} %get-tuple-element.89), channel_id=1, source_target_pairs={{0,16},{16,0},{1,17},{17,1},{2,18},{18,2},{3,19},{19,3},{4,20},{20... | collective-permute-start | bytes 651272 | tf_op jit(solution)/shard_map/ppermute | solution.py:429
  208.2 8.2 %collective-permute-start.34 = (f32[424,128]{1,0:T(8,128)S(1)}, f32[424,128]{1,0:T(8,128)S(1)}, u32[]{:S(2)}, u32[]{:S(2)}) collective-permute-start(f32[424,128]{1,0:T(8,128)S(1)} %get-tuple-element.89), channel_id=1, source_target_pairs={{0,1},{1,0},{2,3},{3,2},{4,5},{5,4},{6,7},{7,6},{8,9},{9,8},{10,11... | collective-permute-start | bytes 651272 | tf_op jit(solution)/shard_map/ppermute | solution.py:429
  208.3 11.3 %collective-permute-start.32 = (f32[424,128]{1,0:T(8,128)S(1)}, f32[424,128]{1,0:T(8,128)S(1)}, u32[]{:S(2)}, u32[]{:S(2)}) collective-permute-start(f32[424,128]{1,0:T(8,128)S(1)} %get-tuple-element.90), channel_id=1, source_target_pairs={{0,16},{16,0},{1,17},{17,1},{2,18},{18,2},{3,19},{19,3},{4,20},{20... | collective-permute-start | bytes 651272 | tf_op jit(solution)/shard_map/ppermute | solution.py:429
  208.8 11.2 %collective-permute-start.31 = (f32[424,128]{1,0:T(8,128)S(1)}, f32[424,128]{1,0:T(8,128)S(1)}, u32[]{:S(2)}, u32[]{:S(2)}) collective-permute-start(f32[424,128]{1,0:T(8,128)S(1)} %get-tuple-element.90), channel_id=1, source_target_pairs={{0,1},{1,0},{2,3},{3,2},{4,5},{5,4},{6,7},{7,6},{8,9},{9,8},{10,11... | collective-permute-start | bytes 651272 | tf_op jit(solution)/shard_map/ppermute | solution.py:429
  215.0 11.9 %copy-start.6 = (f32[424,128]{1,0:T(8,128)}, f32[424,128]{1,0:T(8,128)S(1)}, u32[]{:S(2)}) copy-start(f32[424,128]{1,0:T(8,128)S(1)} %collective-permute-done.35.refs_4_) | copy-start | bytes 651268
  215.0 5.0 %collective-permute-start.41 = (f32[424,128]{1,0:T(8,128)S(1)}, f32[424,128]{1,0:T(8,128)S(1)}, u32[]{:S(2)}, u32[]{:S(2)}) collective-permute-start(f32[424,128]{1,0:T(8,128)S(1)} %collective-permute-done.35.refs_4_), channel_id=1, source_target_pairs={{0,4},{4,0},{8,12},{12,8},{1,5},{5,1},{9,13},{13,9},{2,6},{6,2},{1... | collective-permute-start | bytes 651272 | tf_op jit(solution)/shard_map/ppermute | solution.py:429
  216.5 10.4 %copy-start.7 = (f32[424,128]{1,0:T(8,128)}, f32[424,128]{1,0:T(8,128)S(1)}, u32[]{:S(2)}) copy-start(f32[424,128]{1,0:T(8,128)S(1)} %collective-permute-done.34.refs_3_) | copy-start | bytes 651268
  216.5 7.0 %collective-permute-start.36 = (f32[424,128]{1,0:T(8,128)S(1)}, f32[424,128]{1,0:T(8,128)S(1)}, u32[]{:S(2)}, u32[]{:S(2)}) collective-permute-start(f32[424,128]{1,0:T(8,128)S(1)} %collective-permute-done.34.refs_3_), channel_id=1, source_target_pairs={{0,16},{16,0},{1,17},{17,1},{2,18},{18,2},{3,19},{19,3},{4,20},{20... | collective-permute-start | bytes 651272 | tf_op jit(solution)/shard_map/ppermute | solution.py:429
  219.5 7.4 %copy-start.8 = (f32[424,128]{1,0:T(8,128)}, f32[424,128]{1,0:T(8,128)S(1)}, u32[]{:S(2)}) copy-start(f32[424,128]{1,0:T(8,128)S(1)} %collective-permute-done.32.refs_1_) | copy-start | bytes 651268
  219.5 5.9 %collective-permute-start.33 = (f32[424,128]{1,0:T(8,128)S(1)}, f32[424,128]{1,0:T(8,128)S(1)}, u32[]{:S(2)}, u32[]{:S(2)}) collective-permute-start(f32[424,128]{1,0:T(8,128)S(1)} %collective-permute-done.32.refs_1_), channel_id=1, source_target_pairs={{0,1},{1,0},{2,3},{3,2},{4,5},{5,4},{6,7},{7,6},{8,9},{9,8},{10,11... | collective-permute-start | bytes 651272 | tf_op jit(solution)/shard_map/ppermute | solution.py:429
  219.5 5.9 %collective-permute-start.40 = (f32[424,128]{1,0:T(8,128)S(1)}, f32[424,128]{1,0:T(8,128)S(1)}, u32[]{:S(2)}, u32[]{:S(2)}) collective-permute-start(f32[424,128]{1,0:T(8,128)S(1)} %collective-permute-done.34.refs_3_), channel_id=1, source_target_pairs={{0,4},{4,0},{8,12},{12,8},{1,5},{5,1},{9,13},{13,9},{2,6},{6,2},{1... | collective-permute-start | bytes 651272 | tf_op jit(solution)/shard_map/ppermute | solution.py:429
  220.0 6.9 %copy-start.9 = (f32[424,128]{1,0:T(8,128)}, f32[424,128]{1,0:T(8,128)S(1)}, u32[]{:S(2)}) copy-start(f32[424,128]{1,0:T(8,128)S(1)} %collective-permute-done.31.refs_0_) | copy-start | bytes 651268
  220.0 5.4 %collective-permute-start.38 = (f32[424,128]{1,0:T(8,128)S(1)}, f32[424,128]{1,0:T(8,128)S(1)}, u32[]{:S(2)}, u32[]{:S(2)}) collective-permute-start(f32[424,128]{1,0:T(8,128)S(1)} %collective-permute-done.32.refs_1_), channel_id=1, source_target_pairs={{0,4},{4,0},{8,12},{12,8},{1,5},{5,1},{9,13},{13,9},{2,6},{6,2},{1... | collective-permute-start | bytes 651272 | tf_op jit(solution)/shard_map/ppermute | solution.py:429
  220.1 6.9 %copy-start.10 = (f32[424,128]{1,0:T(8,128)}, f32[424,128]{1,0:T(8,128)S(1)}, u32[]{:S(2)}) copy-start(f32[424,128]{1,0:T(8,128)S(1)} %collective-permute-done.41.refs_10_) | copy-start | bytes 651268
  220.1 5.4 %collective-permute-start.37 = (f32[424,128]{1,0:T(8,128)S(1)}, f32[424,128]{1,0:T(8,128)S(1)}, u32[]{:S(2)}, u32[]{:S(2)}) collective-permute-start(f32[424,128]{1,0:T(8,128)S(1)} %collective-permute-done.31.refs_0_), channel_id=1, source_target_pairs={{0,4},{4,0},{8,12},{12,8},{1,5},{5,1},{9,13},{13,9},{2,6},{6,2},{1... | collective-permute-start | bytes 651272 | tf_op jit(solution)/shard_map/ppermute | solution.py:429
  223.5 3.5 %copy-start.11 = (f32[424,128]{1,0:T(8,128)}, f32[424,128]{1,0:T(8,128)S(1)}, u32[]{:S(2)}) copy-start(f32[424,128]{1,0:T(8,128)S(1)} %collective-permute-done.36.refs_5_) | copy-start | bytes 651268
  223.5 2.0 collective-permute-start.42
  225.4 1.5 copy-start.12
  225.4 1.5 collective-permute-start.39
  225.4 1.5 copy-start.13
  225.4 1.5 copy-start.14
  225.5 1.5 copy-start.15
  225.5 1.5 copy-start.16
  (1 other events, 0.7 us)
where the time goes:
time: 232 us
  waiting for transfers between devices  97.9 us (42%)
  Pallas kernels  80.2 us (35%)
  starting transfers between devices  35 us (15%)
  other arithmetic  13.1 us (6%)
  local copies, waits for them, and re-layouts  4.87 us (2%)
    ppermute x36, waiting for transfers between devices, swap(): return lax.ppermute(value, axis, [(i, i ^ bit) for i in range(size)])  95.7 us
    pallas_call x1, Pallas kernels, solve(): pl.pallas_call(functools.partial(solve_kernel, all_rows, walkers, width_i...  45.9 us
    ppermute x36, starting transfers between devices, swap(): return lax.ppermute(value, axis, [(i, i ^ bit) for i in range(size)])  25.3 us
    pallas_call x2, Pallas kernels, factor_sums(): pl.pallas_call(factor_kernel, out_shape=(out, out), grid_spec=pltpu.Prefe...  19.8 us
    pallas_call x1, Pallas kernels, grad_sums(): pl.pallas_call(grad_kernel, out_shape=(out, out), grid_spec=pltpu.Prefetc...  10.5 us
    ppermute x7, starting transfers between devices, along(): lax.ppermute(value, axes, [(i, (i + k) % size) for i in range(size)])  9.74 us
  transfers between devices with their start and end apart: 43, of which 22 were waited for; matrix products, arithmetic and copies ran while one was open for 6% of the time, Pallas kernels for 13%

commit v1 on v0

--- a/solution.py
+++ b/solution.py
@@ -54,10 +54,13 @@
     tail = width_in % LANES
     rows = keep_ref.shape[1]
 
-    def panel(o_ref, i, start):
+    _, second = layout(width_in, width_out)
+    strips = len(second) * LANES
+
+    def panel(o_ref, tail_ref, i, start):
         lo = i * LANES
         hi = min(i + 2, full) * LANES
-        sums = outer(x_ref[0, lo : full * LANES, :], x_ref[0, lo:hi, :])
+        sums = outer(x_ref[0, lo:, :], x_ref[0, lo:hi, :])
         at = start
         for b in range((hi - lo) // LANES):
             for j in range(b, full - i):
@@ -65,46 +68,44 @@
                     j * LANES : (j + 1) * LANES, b * LANES : (b + 1) * LANES
                 ]
                 at += LANES
+            if tail:
+                row = strips + (i + b) * tail
+                tail_ref[0, row : row + tail, :] = sums[
+                    full * LANES - lo :, b * LANES : (b + 1) * LANES
+                ]
         return at
 
-    def first_half(o_ref):
-        at = panel(o_ref, 0, 0)
+    def halves(one_ref, two_ref):
+        at = panel(one_ref, two_ref, 0, 0)
         sums = gram(g_ref[0], g_ref[0])
         for i in range(width_out // LANES):
             for j in range(i, width_out // LANES):
-                o_ref[0, at : at + LANES, :] = sums[
+                one_ref[0, at : at + LANES, :] = sums[
                     j * LANES : (j + 1) * LANES, i * LANES : (i + 1) * LANES
                 ]
                 at += LANES
         if at < rows:
-            o_ref[0, at:, :] = jnp.zeros((rows - at, LANES), F32)
-
-    def second_half(o_ref):
+            one_ref[0, at:, :] = jnp.zeros((rows - at, LANES), F32)
         at = 0
         for i in range(2, full, 2):
-            at = panel(o_ref, i, at)
+            at = panel(two_ref, two_ref, i, at)
+        at = strips
         if tail:
             last = x_ref[0, full * LANES :, :]
-            strip = outer(last, x_ref[0, : full * LANES, :])
-            for j in range(full):
-                o_ref[0, at : at + tail, :] = strip[:, j * LANES : (j + 1) * LANES]
-                at += tail
-            corner = outer(last, last)
-            o_ref[0, at : at + tail, :] = jnp.zeros((tail, LANES), F32)
-            o_ref[0, at : at + tail, :tail] = corner
+            at += full * tail
+            two_ref[0, at : at + tail, :] = jnp.zeros((tail, LANES), F32)
+            two_ref[0, at : at + tail, :tail] = outer(last, last)
             at += tail
         if at < rows:
-            o_ref[0, at:, :] = jnp.zeros((rows - at, LANES), F32)
+            two_ref[0, at:, :] = jnp.zeros((rows - at, LANES), F32)
 
     @pl.when(where_ref[0] == 0)
     def _():
-        first_half(keep_ref)
-        second_half(send_ref)
+        halves(keep_ref, send_ref)
 
     @pl.when(where_ref[0] == 1)
     def _():
-        first_half(send_ref)
-        second_half(keep_ref)
+        halves(send_ref, keep_ref)
 
 
 def factor_sums(where, first, layers, x, g):
@@ -554,9 +555,8 @@
         for which in back:
             mine = bit_of(*bits[which])
             other = swap(piece, *bits[which])
-            low = jnp.where(mine == 0, piece, other)
-            high = jnp.where(mine == 0, other, piece)
-            piece = jnp.stack([low, high])
+            index = lax.broadcasted_iota(jnp.int32, (2,) + piece.shape, 0)
+            piece = jnp.where(index == mine, piece[None], other[None])
             dims.insert(0, which)
         rank = len(dims)
         axes = sorted(range(rank), key=lambda k: dims[k])

time: 232 us -> 211 us (0.909)
  waiting for transfers between devices: 97.9 us -> 77.9 us
  other arithmetic: 13.1 us -> 9.59 us
  starting transfers between devices: 35 us -> 38.3 us
    ppermute x36, waiting for transfers between devices: 95.7 us -> 75.7 us  [swap(): return lax.ppermute(value, axis, [(i, i ^ bit) for i in range(size)])]
    ppermute x36, starting transfers between devices: 25.3 us -> 28.6 us  [swap(): return lax.ppermute(value, axis, [(i, i ^ bit) for i in range(size)])]
  transfers between devices with their start and end apart: 43 -> 43, of which waited for: 22 -> 25; matrix products, arithmetic and copies ran while one was open for 6% -> 5% of each run, Pallas kernels for 13% -> 13%
where the time goes in v1:
time: 211 us
  Pallas kernels  78.1 us (37%)
  waiting for transfers between devices  77.9 us (37%)
  starting transfers between devices  38.3 us (18%)
  other arithmetic  9.59 us (5%)
  local copies, waits for them, and re-layouts  6.42 us (3%)
    ppermute x36, waiting for transfers between devices, swap(): return lax.ppermute(value, axis, [(i, i ^ bit) for i in range(size)])  75.7 us
    pallas_call x1, Pallas kernels, solve(): pl.pallas_call(functools.partial(solve_kernel, all_rows, walkers, width_i...  45.9 us
    ppermute x36, starting transfers between devices, swap(): return lax.ppermute(value, axis, [(i, i ^ bit) for i in range(size)])  28.6 us
    pallas_call x2, Pallas kernels, factor_sums(): pl.pallas_call(factor_kernel, out_shape=(out, out), grid_spec=pltpu.Prefe...  17.8 us
    pallas_call x1, Pallas kernels, grad_sums(): pl.pallas_call(grad_kernel, out_shape=(out, out), grid_spec=pltpu.Prefetc...  10.5 us
    ppermute x7, starting transfers between devices, along(): lax.ppermute(value, axes, [(i, (i + k) % size) for i in range(size)])  9.75 us
  transfers between devices with their start and end apart: 43, of which 25 were waited for; matrix products, arithmetic and copies ran while one was open for 5% of the time, Pallas kernels for 13%

profile of v1, /device:TPU:0, one launch (start us, length us, event | category | flops | bytes accessed | tf_op | source)
XLA Modules:
  0.0 210.8 jit_solution(9649470916907887815)
XLA Ops:
  0.0 1.3 reduce_sum.9
  1.3 0.6 broadcast_in_dim.115
  1.9 5.1 %collective-permute-start.2 = (f32[8,128]{1,0:T(8,128)S(1)}, f32[8,128]{1,0:T(8,128)S(1)}, u32[]{:S(2)}, u32[]{:S(2)}) collective-permute-start(f32[8,128]{1,0:T(8,128)S(1)} %broadcast_in_dim.115), channel_id=1, source_target_pairs={{0,3},{1,0},{2,1},{3,2},{4,7},{5,4},{6,5},{7,6},{8,11},{9,8},{10,9... | collective-permute-start | bytes 12296 | tf_op jit(solution)/shard_map/ppermute | solution.py:476
  7.0 1.0 collective-permute-start
  8.1 0.6 pad_add_fusion.where_ref.core_ref.s_ref
  8.7 8.9 %factor_sums.2 = (f32[2,1792,128]{2,1,0:T(8,128)}, f32[2,1792,128]{2,1,0:T(8,128)}) custom-call(s32[2]{0:T(128)} %pad_add_fusion.where_ref.core_ref.s_ref, bf16[4,832,1920]{2,1,0:T(8,128)(2,1)} %bitcast.126, bf16[4,1920,256]{2,1,0:T(8,128)(2,1)} %g_ref.5), custom_call_target="tpu_custom_call" | custom-call | flops 2658140160 | bytes 12025856 | tf_op jit(solution)/shard_map/factor_sums/pallas_call | solution.py:117
  17.7 1.6 collective-permute-start.5
  19.8 8.9 %factor_sums.3 = (f32[2,1792,128]{2,1,0:T(8,128)}, f32[2,1792,128]{2,1,0:T(8,128)}) custom-call(s32[2]{0:T(128)} %pad_add_fusion.where_ref.core_ref.s_ref, bf16[4,832,1920]{2,1,0:T(8,128)(2,1)} %bitcast.127, bf16[4,1920,256]{2,1,0:T(8,128)(2,1)} %g_ref.5), custom_call_target="tpu_custom_call" | custom-call | flops 2658140160 | bytes 12025856 | tf_op jit(solution)/shard_map/factor_sums/pallas_call | solution.py:117
  28.7 1.7 collective-permute-start.6
  30.4 1.5 collective-permute-start.8
  31.9 2.1 %collective-permute-done.8 = f32[8,128]{1,0:T(8,128)S(1)} collective-permute-done((f32[8,128]{1,0:T(8,128)S(1)}, f32[8,128]{1,0:T(8,128)S(1)}, u32[]{:S(2)}, u32[]{:S(2)}) %collective-permute-start.8) | collective-permute-done | bytes 4128 | tf_op jit(solution)/shard_map/ppermute | solution.py:476
  34.2 1.0 reshape.200.c_ref
  35.2 2.2 %slice_add_fusion = f32[2,896,128]{2,1,0:T(8,128)} fusion(f32[2,1792,128]{2,1,0:T(8,128)} %collective-permute-done.7, f32[2,1792,128]{2,1,0:T(8,128)S(1)} %copy-done), kind=kLoop, calls=%fused_computation | loop fusion | flops 229376 | bytes 2752512 | tf_op jit(solution)/shard_map/add | solution.py:514
  37.4 1.5 collective-permute-start.9
  38.9 10.5 %grad_sums.1 = (f32[4,832,128]{2,1,0:T(8,128)}, f32[4,832,128]{2,1,0:T(8,128)}) custom-call(s32[2]{0:T(128)} %pad_add_fusion.where_ref.core_ref.s_ref, bf16[4,832,1920]{2,1,0:T(8,128)(2,1)} %bitcast.128, bf16[4,1920,256]{2,1,0:T(8,128)(2,1)} %g_ref.5, f32[1920,128]{1,0:T(8,128)} %reshape.200.c_ref), custom_call_target="tpu_custom_call" | custom-call | flops 3271557120 | bytes 20119552 | tf_op jit(solution)/shard_map/grad_sums/pallas_call | solution.py:162
  49.4 1.4 slice_add_fusion.3
  51.2 1.1 copy-done.1
  52.3 1.3 slice_add_fusion.5
  53.7 2.5 %collective-permute-start.15 = (f32[2,2,2,224,128]{4,3,2,1,0:T(8,128)S(1)}, f32[2,2,2,224,128]{4,3,2,1,0:T(8,128)S(1)}, u32[]{:S(2)}, u32[]{:S(2)}) collective-permute-start(f32[2,2,2,224,128]{4,3,2,1,0:T(8,128)S(1)} %pad_maximum_fusion), channel_id=1, source_target_pairs={{0,1},{1,0},{2,3},{3,2},{4,5},{5,4},{6,7},{7,6},{8,9},{9,8},{10,11... | collective-permute-start | bytes 2752520 | tf_op jit(solution)/shard_map/ppermute | solution.py:430
  56.2 1.3 slice_add_fusion.1
  57.6 1.2 collective-permute-done.9
  58.9 2.5 %collective-permute-start.10 = (f32[2,2,224,128]{3,2,1,0:T(8,128)S(1)}, f32[2,2,224,128]{3,2,1,0:T(8,128)S(1)}, u32[]{:S(2)}, u32[]{:S(2)}) collective-permute-start(f32[2,2,224,128]{3,2,1,0:T(8,128)S(1)} %get-tuple-element.78), channel_id=1, source_target_pairs={{0,1},{1,0},{2,3},{3,2},{4,5},{5,4},{6,7},{7,6},{8,9},{9,8},{10,11... | collective-permute-start | bytes 1376264 | tf_op jit(solution)/shard_map/ppermute | solution.py:430
  61.8 0.6 collective-permute-start.22
  62.4 15.1 %collective-permute-done.15 = f32[2,2,2,224,128]{4,3,2,1,0:T(8,128)S(1)} collective-permute-done((f32[2,2,2,224,128]{4,3,2,1,0:T(8,128)S(1)}, f32[2,2,2,224,128]{4,3,2,1,0:T(8,128)S(1)}, u32[]{:S(2)}, u32[]{:S(2)}) %collective-permute-start.15) | collective-permute-done | bytes 917536 | tf_op jit(solution)/shard_map/ppermute | solution.py:430
  77.5 0.6 collective-permute-start.16
  78.1 8.7 %collective-permute-done.10 = f32[2,2,224,128]{3,2,1,0:T(8,128)S(1)} collective-permute-done((f32[2,2,224,128]{3,2,1,0:T(8,128)S(1)}, f32[2,2,224,128]{3,2,1,0:T(8,128)S(1)}, u32[]{:S(2)}, u32[]{:S(2)}) %collective-permute-start.10) | collective-permute-done | bytes 458784 | tf_op jit(solution)/shard_map/ppermute | solution.py:430
  86.9 0.6 collective-permute-start.11
  87.5 1.8 collective-permute-done.16
  89.4 0.6 collective-permute-start.17
  90.1 1.5 collective-permute-start.23
  91.7 3.8 %collective-permute-done.11 = f32[2,224,128]{2,1,0:T(8,128)S(1)} collective-permute-done((f32[2,224,128]{2,1,0:T(8,128)S(1)}, f32[2,224,128]{2,1,0:T(8,128)S(1)}, u32[]{:S(2)}, u32[]{:S(2)}) %collective-permute-start.11) | collective-permute-done | bytes 229408 | tf_op jit(solution)/shard_map/ppermute | solution.py:430
  95.5 1.2 collective-permute-start.12
  96.7 2.4 %collective-permute-done.17 = f32[2,224,128]{2,1,0:T(8,128)S(1)} collective-permute-done((f32[2,224,128]{2,1,0:T(8,128)S(1)}, f32[2,224,128]{2,1,0:T(8,128)S(1)}, u32[]{:S(2)}, u32[]{:S(2)}) %collective-permute-start.17) | collective-permute-done | bytes 229408 | tf_op jit(solution)/shard_map/ppermute | solution.py:430
  99.2 1.0 collective-permute-start.18
  100.1 2.9 %collective-permute-done.23 = f32[2,2,208,128]{3,2,1,0:T(8,128)S(1)} collective-permute-done((f32[2,2,208,128]{3,2,1,0:T(8,128)S(1)}, f32[2,2,208,128]{3,2,1,0:T(8,128)S(1)}, u32[]{:S(2)}, u32[]{:S(2)}) %collective-permute-start.23) | collective-permute-done | bytes 426016 | tf_op jit(solution)/shard_map/ppermute | solution.py:430
  103.1 0.6 collective-permute-start.24
  103.7 3.2 %collective-permute-start.13 = (f32[224,128]{1,0:T(8,128)S(1)}, f32[224,128]{1,0:T(8,128)S(1)}, u32[]{:S(2)}, u32[]{:S(2)}) collective-permute-start(f32[224,128]{1,0:T(8,128)S(1)} %bitcast_add_fusion.7), channel_id=1, source_target_pairs={{0,2},{1,3},{2,0},{3,1},{4,6},{5,7},{6,4},{7,5},{8,10},{9,11},{10,... | collective-permute-start | bytes 344072 | tf_op jit(solution)/shard_map/ppermute | solution.py:430
  107.0 2.1 collective-permute-done.24
  109.1 2.5 %collective-permute-done.18 = f32[224,128]{1,0:T(8,128)S(1)} collective-permute-done((f32[224,128]{1,0:T(8,128)S(1)}, f32[224,128]{1,0:T(8,128)S(1)}, u32[]{:S(2)}, u32[]{:S(2)}) %collective-permute-start.18) | collective-permute-done | bytes 114720 | tf_op jit(solution)/shard_map/ppermute | solution.py:430
  112.1 7.9 %collective-permute-done.25 = f32[208,128]{1,0:T(8,128)S(1)} collective-permute-done((f32[208,128]{1,0:T(8,128)S(1)}, f32[208,128]{1,0:T(8,128)S(1)}, u32[]{:S(2)}, u32[]{:S(2)}) %collective-permute-start.25) | collective-permute-done | bytes 106528 | tf_op jit(solution)/shard_map/ppermute | solution.py:430
  120.0 0.9 collective-permute-start.26
  120.9 1.2 collective-permute-done.19
  122.2 0.6 collective-permute-start.20
  122.8 1.5 collective-permute-start.14
  124.3 0.6 collective-permute-done.26
  125.3 5.5 %collective-permute-done.20 = f32[2,224,128]{2,1,0:T(8,128)S(1)} collective-permute-done((f32[2,224,128]{2,1,0:T(8,128)S(1)}, f32[2,224,128]{2,1,0:T(8,128)S(1)}, u32[]{:S(2)}, u32[]{:S(2)}) %collective-permute-start.20) | collective-permute-done | bytes 229408 | tf_op jit(solution)/shard_map/ppermute | solution.py:430
  130.8 3.9 %collective-permute-done.14 = f32[2,224,128]{2,1,0:T(8,128)S(1)} collective-permute-done((f32[2,224,128]{2,1,0:T(8,128)S(1)}, f32[2,224,128]{2,1,0:T(8,128)S(1)}, u32[]{:S(2)}, u32[]{:S(2)}) %collective-permute-start.14) | collective-permute-done | bytes 229408 | tf_op jit(solution)/shard_map/ppermute | solution.py:430
  135.9 0.8 collective-permute-done.29.got1
  136.7 0.7 collective-permute-done.28.got0
  137.4 0.6 collective-permute-done.30.got2
  138.2 0.8 copy-done.21
  138.9 45.9 %solve.1 = (f32[2,424,128]{2,1,0:T(8,128)}, f32[832,128]{1,0:T(8,128)}) custom-call(s32[2]{0:T(128)} %pad_add_fusion.where_ref.core_ref.s_ref, f32[896,128]{1,0:T(8,128)} %copy-done.4, f32[896,128]{1,0:T(8,128)} %copy-done.3, f32[832,128]{1,0:T(8,128)} %copy-done.5, f32[896,128]{1,0:T(8,128)} %copy-done.20, f32[896,128]{1,0:T(8,128)} %copy-done.19, ...), custom_call_target="tpu_custom_call" | custom-call | flops 10632560640 | bytes 4194304 | tf_op jit(solution)/shard_map/solve/pallas_call | solution.py:377
  184.8 1.1 slice_bitcast_fusion.4
  185.9 0.6 collective-permute-start.35
  186.5 1.5 collective-permute-start.32
  188.0 2.0 collective-permute-start.31
  190.0 4.2 %collective-permute-done.35.refs_4_ = f32[424,128]{1,0:T(8,128)S(1)} collective-permute-done((f32[424,128]{1,0:T(8,128)S(1)}, f32[424,128]{1,0:T(8,128)S(1)}, u32[]{:S(2)}, u32[]{:S(2)}) %collective-permute-start.35) | collective-permute-done | bytes 217120 | tf_op jit(solution)/shard_map/ppermute | solution.py:430
  194.7 1.5 collective-permute-start.36
  196.2 2.6 %collective-permute-done.32.refs_1_ = f32[424,128]{1,0:T(8,128)S(1)} collective-permute-done((f32[424,128]{1,0:T(8,128)S(1)}, f32[424,128]{1,0:T(8,128)S(1)}, u32[]{:S(2)}, u32[]{:S(2)}) %collective-permute-start.32) | collective-permute-done | bytes 217120 | tf_op jit(solution)/shard_map/ppermute | solution.py:430
  199.4 3.3 %collective-permute-done.36.refs_5_ = f32[424,128]{1,0:T(8,128)S(1)} collective-permute-done((f32[424,128]{1,0:T(8,128)S(1)}, f32[424,128]{1,0:T(8,128)S(1)}, u32[]{:S(2)}, u32[]{:S(2)}) %collective-permute-start.36) | collective-permute-done | bytes 217120 | tf_op jit(solution)/shard_map/ppermute | solution.py:430
  202.7 2.0 collective-permute-done.33.refs_2_
  204.8 1.4 collective-permute-done.39.refs_8_
  206.3 0.6 copy-done.17
  206.9 4.0 %finish.1 = f32[4,832,256]{2,1,0:T(8,128)} custom-call(s32[2]{0:T(128)} %pad_add_fusion.where_ref.core_ref.s_ref, f32[2,424,128]{2,1,0:T(8,128)} %get-tuple-element.57.mine, f32[832,128]{1,0:T(8,128)} %get-tuple-element.58.other, f32[424,128]{1,0:T(8,128)} %copy-done.9, f32[424,128]{1,0:T(8,128)} %copy-done.8, f32[424,128]{1,0:T(8,128)} %copy-done.12, ...), custom_call_target="tpu_custom_call" | custom-call | tf_op jit(solution)/shard_map/finish/pallas_call | solution.py:418
  (116 shorter events, 5.9 us)
Async XLA Ops:
  1.9 15.7 %collective-permute-start.2 = (f32[8,128]{1,0:T(8,128)S(1)}, f32[8,128]{1,0:T(8,128)S(1)}, u32[]{:S(2)}, u32[]{:S(2)}) collective-permute-start(f32[8,128]{1,0:T(8,128)S(1)} %broadcast_in_dim.115), channel_id=1, source_target_pairs={{0,3},{1,0},{2,1},{3,2},{4,7},{5,4},{6,5},{7,6},{8,11},{9,8},{10,9... | collective-permute-start | bytes 12296 | tf_op jit(solution)/shard_map/ppermute | solution.py:476
  7.0 10.5 %collective-permute-start.1 = (f32[8,128]{1,0:T(8,128)S(1)}, f32[8,128]{1,0:T(8,128)S(1)}, u32[]{:S(2)}, u32[]{:S(2)}) collective-permute-start(f32[8,128]{1,0:T(8,128)S(1)} %broadcast_in_dim.115), channel_id=1, source_target_pairs={{0,2},{1,3},{2,0},{3,1},{4,6},{5,7},{6,4},{7,5},{8,10},{9,11},{10,... | collective-permute-start | bytes 12296 | tf_op jit(solution)/shard_map/ppermute | solution.py:476
  7.0 10.5 %collective-permute-start = (f32[8,128]{1,0:T(8,128)S(1)}, f32[8,128]{1,0:T(8,128)S(1)}, u32[]{:S(2)}, u32[]{:S(2)}) collective-permute-start(f32[8,128]{1,0:T(8,128)S(1)} %broadcast_in_dim.115), channel_id=1, source_target_pairs={{0,1},{1,2},{2,3},{3,0},{4,5},{5,6},{6,7},{7,4},{8,9},{9,10},{10,1... | collective-permute-start | bytes 12296 | tf_op jit(solution)/shard_map/ppermute | solution.py:476
  17.6 17.6 %collective-permute-start.7 = (f32[2,1792,128]{2,1,0:T(8,128)}, f32[2,1792,128]{2,1,0:T(8,128)}, u32[]{:S(2)}, u32[]{:S(2)}) collective-permute-start(f32[2,1792,128]{2,1,0:T(8,128)} %get-tuple-element.46), channel_id=1, source_target_pairs={{0,4},{4,0},{8,12},{12,8},{1,5},{5,1},{9,13},{13,9},{2,6},{6,2},{1... | collective-permute-start | bytes 5505032 | tf_op jit(solution)/shard_map/ppermute | solution.py:430
  17.7 16.3 %copy-start.18 = (f32[32]{0:T(128)S(1)}, f32[32]{0:T(128)}, u32[]{:S(2)}) copy-start(f32[32]{0:T(128)} %param.5) | copy-start | bytes 388
  17.7 11.0 %collective-permute-start.5 = (f32[8,128]{1,0:T(8,128)S(1)}, f32[8,128]{1,0:T(8,128)S(1)}, u32[]{:S(2)}, u32[]{:S(2)}) collective-permute-start(f32[8,128]{1,0:T(8,128)S(1)} %add_add_fusion.1), channel_id=1, source_target_pairs={{0,12},{4,0},{8,4},{12,8},{1,13},{5,1},{9,5},{13,9},{2,14},{6,2},{... | collective-permute-start | bytes 12296 | tf_op jit(solution)/shard_map/ppermute | solution.py:476
  19.3 9.4 %collective-permute-start.4 = (f32[8,128]{1,0:T(8,128)S(1)}, f32[8,128]{1,0:T(8,128)S(1)}, u32[]{:S(2)}, u32[]{:S(2)}) collective-permute-start(f32[8,128]{1,0:T(8,128)S(1)} %add_add_fusion.1), channel_id=1, source_target_pairs={{0,8},{4,12},{8,0},{12,4},{1,9},{5,13},{9,1},{13,5},{2,10},{6,14},... | collective-permute-start | bytes 12296 | tf_op jit(solution)/shard_map/ppermute | solution.py:476
  19.8 8.9 %collective-permute-start.3 = (f32[8,128]{1,0:T(8,128)S(1)}, f32[8,128]{1,0:T(8,128)S(1)}, u32[]{:S(2)}, u32[]{:S(2)}) collective-permute-start(f32[8,128]{1,0:T(8,128)S(1)} %add_add_fusion.1), channel_id=1, source_target_pairs={{0,4},{4,8},{8,12},{12,0},{1,5},{5,9},{9,13},{13,1},{2,6},{6,10},{... | collective-permute-start | bytes 12296 | tf_op jit(solution)/shard_map/ppermute | solution.py:476
  28.7 6.5 %copy-start = (f32[2,1792,128]{2,1,0:T(8,128)S(1)}, f32[2,1792,128]{2,1,0:T(8,128)}, u32[]{:S(2)}) copy-start(f32[2,1792,128]{2,1,0:T(8,128)} %get-tuple-element.45) | copy-start | bytes 5505028
  28.7 22.5 %collective-permute-start.6 = (f32[2,1792,128]{2,1,0:T(8,128)}, f32[2,1792,128]{2,1,0:T(8,128)}, u32[]{:S(2)}, u32[]{:S(2)}) collective-permute-start(f32[2,1792,128]{2,1,0:T(8,128)} %get-tuple-element.44), channel_id=1, source_target_pairs={{0,4},{4,0},{8,12},{12,8},{1,5},{5,1},{9,13},{13,9},{2,6},{6,2},{1... | collective-permute-start | bytes 5505032 | tf_op jit(solution)/shard_map/ppermute | solution.py:430
  30.4 3.6 %collective-permute-start.8 = (f32[8,128]{1,0:T(8,128)S(1)}, f32[8,128]{1,0:T(8,128)S(1)}, u32[]{:S(2)}, u32[]{:S(2)}) collective-permute-start(f32[8,128]{1,0:T(8,128)S(1)} %add_add_fusion), channel_id=1, source_target_pairs={{0,16},{16,0},{1,17},{17,1},{2,18},{18,2},{3,19},{19,3},{4,20},{20... | collective-permute-start | bytes 12296 | tf_op jit(solution)/shard_map/ppermute | solution.py:476
  37.4 21.4 %collective-permute-start.9 = (f32[2,2,2,224,128]{4,3,2,1,0:T(8,128)}, f32[2,2,2,224,128]{4,3,2,1,0:T(8,128)S(1)}, u32[]{:S(2)}, u32[]{:S(2)}) collective-permute-start(f32[2,2,2,224,128]{4,3,2,1,0:T(8,128)} %bitcast.5), channel_id=1, source_target_pairs={{0,16},{16,0},{1,17},{17,1},{2,18},{18,2},{3,19},{19,3},{4,20},{20... | collective-permute-start | bytes 2752520 | tf_op jit(solution)/shard_map/ppermute | solution.py:430
  49.3 1.7 copy-start.2
  49.3 12.1 %collective-permute-start.21 = (f32[4,832,128]{2,1,0:T(8,128)}, f32[4,832,128]{2,1,0:T(8,128)S(1)}, u32[]{:S(2)}, u32[]{:S(2)}) collective-permute-start(f32[4,832,128]{2,1,0:T(8,128)} %get-tuple-element.56), channel_id=1, source_target_pairs={{0,4},{4,0},{8,12},{12,8},{1,5},{5,1},{9,13},{13,9},{2,6},{6,2},{1... | collective-permute-start | bytes 5111816 | tf_op jit(solution)/shard_map/ppermute | solution.py:430
  50.7 1.6 copy-start.1
  53.7 23.7 %collective-permute-start.15 = (f32[2,2,2,224,128]{4,3,2,1,0:T(8,128)S(1)}, f32[2,2,2,224,128]{4,3,2,1,0:T(8,128)S(1)}, u32[]{:S(2)}, u32[]{:S(2)}) collective-permute-start(f32[2,2,2,224,128]{4,3,2,1,0:T(8,128)S(1)} %pad_maximum_fusion), channel_id=1, source_target_pairs={{0,1},{1,0},{2,3},{3,2},{4,5},{5,4},{6,7},{7,6},{8,9},{9,8},{10,11... | collective-permute-start | bytes 2752520 | tf_op jit(solution)/shard_map/ppermute | solution.py:430
  58.9 28.0 %collective-permute-start.10 = (f32[2,2,224,128]{3,2,1,0:T(8,128)S(1)}, f32[2,2,224,128]{3,2,1,0:T(8,128)S(1)}, u32[]{:S(2)}, u32[]{:S(2)}) collective-permute-start(f32[2,2,224,128]{3,2,1,0:T(8,128)S(1)} %get-tuple-element.78), channel_id=1, source_target_pairs={{0,1},{1,0},{2,3},{3,2},{4,5},{5,4},{6,7},{7,6},{8,9},{9,8},{10,11... | collective-permute-start | bytes 1376264 | tf_op jit(solution)/shard_map/ppermute | solution.py:430
  61.8 28.2 %collective-permute-start.22 = (f32[2,2,2,208,128]{4,3,2,1,0:T(8,128)S(1)}, f32[2,2,2,208,128]{4,3,2,1,0:T(8,128)S(1)}, u32[]{:S(2)}, u32[]{:S(2)}) collective-permute-start(f32[2,2,2,208,128]{4,3,2,1,0:T(8,128)S(1)} %pad_maximum_fusion.1), channel_id=1, source_target_pairs={{0,8},{4,12},{8,0},{12,4},{1,9},{5,13},{9,1},{13,5},{2,10},{6,14},... | collective-permute-start | bytes 2555912 | tf_op jit(solution)/shard_map/ppermute | solution.py:430
  77.5 11.8 %collective-permute-start.16 = (f32[2,2,224,128]{3,2,1,0:T(8,128)S(1)}, f32[2,2,224,128]{3,2,1,0:T(8,128)S(1)}, u32[]{:S(2)}, u32[]{:S(2)}) collective-permute-start(f32[2,2,224,128]{3,2,1,0:T(8,128)S(1)} %get-tuple-element.74), channel_id=1, source_target_pairs={{0,16},{16,0},{1,17},{17,1},{2,18},{18,2},{3,19},{19,3},{4,20},{20... | collective-permute-start | bytes 1376264 | tf_op jit(solution)/shard_map/ppermute | solution.py:430
  86.9 8.5 %collective-permute-start.11 = (f32[2,224,128]{2,1,0:T(8,128)S(1)}, f32[2,224,128]{2,1,0:T(8,128)S(1)}, u32[]{:S(2)}, u32[]{:S(2)}) collective-permute-start(f32[2,224,128]{2,1,0:T(8,128)S(1)} %get-tuple-element.76), channel_id=1, source_target_pairs={{0,8},{4,12},{8,0},{12,4},{1,9},{5,13},{9,1},{13,5},{2,10},{6,14},... | collective-permute-start | bytes 688136 | tf_op jit(solution)/shard_map/ppermute | solution.py:430
  89.4 9.7 %collective-permute-start.17 = (f32[2,224,128]{2,1,0:T(8,128)S(1)}, f32[2,224,128]{2,1,0:T(8,128)S(1)}, u32[]{:S(2)}, u32[]{:S(2)}) collective-permute-start(f32[2,224,128]{2,1,0:T(8,128)S(1)} %get-tuple-element.72), channel_id=1, source_target_pairs={{0,8},{4,12},{8,0},{12,4},{1,9},{5,13},{9,1},{13,5},{2,10},{6,14},... | collective-permute-start | bytes 688136 | tf_op jit(solution)/shard_map/ppermute | solution.py:430
  90.1 12.9 %collective-permute-start.23 = (f32[2,2,208,128]{3,2,1,0:T(8,128)S(1)}, f32[2,2,208,128]{3,2,1,0:T(8,128)S(1)}, u32[]{:S(2)}, u32[]{:S(2)}) collective-permute-start(f32[2,2,208,128]{3,2,1,0:T(8,128)S(1)} %get-tuple-element.64), channel_id=1, source_target_pairs={{0,1},{1,0},{2,3},{3,2},{4,5},{5,4},{6,7},{7,6},{8,9},{9,8},{10,11... | collective-permute-start | bytes 1277960 | tf_op jit(solution)/shard_map/ppermute | solution.py:430
  95.5 8.2 %collective-permute-start.12 = (f32[224,128]{1,0:T(8,128)S(1)}, f32[224,128]{1,0:T(8,128)S(1)}, u32[]{:S(2)}, u32[]{:S(2)}) collective-permute-start(f32[224,128]{1,0:T(8,128)S(1)} %fusion.12), channel_id=1, source_target_pairs={{0,2},{1,3},{2,0},{3,1},{4,6},{5,7},{6,4},{7,5},{8,10},{9,11},{10,... | collective-permute-start | bytes 344072 | tf_op jit(solution)/shard_map/ppermute | solution.py:430
  99.2 12.5 %collective-permute-start.18 = (f32[224,128]{1,0:T(8,128)S(1)}, f32[224,128]{1,0:T(8,128)S(1)}, u32[]{:S(2)}, u32[]{:S(2)}) collective-permute-start(f32[224,128]{1,0:T(8,128)S(1)} %fusion.11), channel_id=1, source_target_pairs={{0,2},{1,3},{2,0},{3,1},{4,6},{5,7},{6,4},{7,5},{8,10},{9,11},{10,... | collective-permute-start | bytes 344072 | tf_op jit(solution)/shard_map/ppermute | solution.py:430
  103.1 5.9 %collective-permute-start.24 = (f32[2,208,128]{2,1,0:T(8,128)S(1)}, f32[2,208,128]{2,1,0:T(8,128)S(1)}, u32[]{:S(2)}, u32[]{:S(2)}) collective-permute-start(f32[2,208,128]{2,1,0:T(8,128)S(1)} %get-tuple-element.82), channel_id=1, source_target_pairs={{0,16},{16,0},{1,17},{17,1},{2,18},{18,2},{3,19},{19,3},{4,20},{20... | collective-permute-start | bytes 638984 | tf_op jit(solution)/shard_map/ppermute | solution.py:430
  103.7 17.2 %collective-permute-start.13 = (f32[224,128]{1,0:T(8,128)S(1)}, f32[224,128]{1,0:T(8,128)S(1)}, u32[]{:S(2)}, u32[]{:S(2)}) collective-permute-start(f32[224,128]{1,0:T(8,128)S(1)} %bitcast_add_fusion.7), channel_id=1, source_target_pairs={{0,2},{1,3},{2,0},{3,1},{4,6},{5,7},{6,4},{7,5},{8,10},{9,11},{10,... | collective-permute-start | bytes 344072 | tf_op jit(solution)/shard_map/ppermute | solution.py:430
  109.0 11.0 %collective-permute-start.25 = (f32[208,128]{1,0:T(8,128)S(1)}, f32[208,128]{1,0:T(8,128)S(1)}, u32[]{:S(2)}, u32[]{:S(2)}) collective-permute-start(f32[208,128]{1,0:T(8,128)S(1)} %fusion.13), channel_id=1, source_target_pairs={{0,2},{1,3},{2,0},{3,1},{4,6},{5,7},{6,4},{7,5},{8,10},{9,11},{10,... | collective-permute-start | bytes 319496 | tf_op jit(solution)/shard_map/ppermute | solution.py:430
  111.7 10.4 %collective-permute-start.19 = (f32[224,128]{1,0:T(8,128)S(1)}, f32[224,128]{1,0:T(8,128)S(1)}, u32[]{:S(2)}, u32[]{:S(2)}) collective-permute-start(f32[224,128]{1,0:T(8,128)S(1)} %bitcast_add_fusion.4), channel_id=1, source_target_pairs={{0,2},{1,3},{2,0},{3,1},{4,6},{5,7},{6,4},{7,5},{8,10},{9,11},{10,... | collective-permute-start | bytes 344072 | tf_op jit(solution)/shard_map/ppermute | solution.py:430
  120.0 4.9 %collective-permute-start.26 = (f32[208,128]{1,0:T(8,128)S(1)}, f32[208,128]{1,0:T(8,128)S(1)}, u32[]{:S(2)}, u32[]{:S(2)}) collective-permute-start(f32[208,128]{1,0:T(8,128)S(1)} %bitcast_add_fusion.10), channel_id=1, source_target_pairs={{0,8},{4,12},{8,0},{12,4},{1,9},{5,13},{9,1},{13,5},{2,10},{6,14},... | collective-permute-start | bytes 319496 | tf_op jit(solution)/shard_map/ppermute | solution.py:430
  122.2 8.5 %collective-permute-start.20 = (f32[2,224,128]{2,1,0:T(8,128)S(1)}, f32[2,224,128]{2,1,0:T(8,128)S(1)}, u32[]{:S(2)}, u32[]{:S(2)}) collective-permute-start(f32[2,224,128]{2,1,0:T(8,128)S(1)} %get-tuple-element.87), channel_id=1, source_target_pairs={{0,8},{4,12},{8,0},{12,4},{1,9},{5,13},{9,1},{13,5},{2,10},{6,14},... | collective-permute-start | bytes 688136 | tf_op jit(solution)/shard_map/ppermute | solution.py:430
  122.8 11.8 %collective-permute-start.14 = (f32[2,224,128]{2,1,0:T(8,128)S(1)}, f32[2,224,128]{2,1,0:T(8,128)S(1)}, u32[]{:S(2)}, u32[]{:S(2)}) collective-permute-start(f32[2,224,128]{2,1,0:T(8,128)S(1)} %get-tuple-element.88), channel_id=1, source_target_pairs={{0,8},{4,12},{8,0},{12,4},{1,9},{5,13},{9,1},{13,5},{2,10},{6,14},... | collective-permute-start | bytes 688136 | tf_op jit(solution)/shard_map/ppermute | solution.py:430
  125.0 10.6 %collective-permute-start.27 = (f32[2,208,128]{2,1,0:T(8,128)S(1)}, f32[2,208,128]{2,1,0:T(8,128)S(1)}, u32[]{:S(2)}, u32[]{:S(2)}) collective-permute-start(f32[2,208,128]{2,1,0:T(8,128)S(1)} %broadcast_select_fusion.2), channel_id=1, source_target_pairs={{0,2},{1,3},{2,0},{3,1},{4,6},{5,7},{6,4},{7,5},{8,10},{9,11},{10,... | collective-permute-start | bytes 638984 | tf_op jit(solution)/shard_map/ppermute | solution.py:430
  134.8 3.2 %copy-start.3 = (f32[896,128]{1,0:T(8,128)}, f32[896,128]{1,0:T(8,128)S(1)}, u32[]{:S(2)}) copy-start(f32[896,128]{1,0:T(8,128)S(1)} %get-tuple-element.85.own1) | copy-start | bytes 1376260
  134.8 3.2 %copy-start.4 = (f32[896,128]{1,0:T(8,128)}, f32[896,128]{1,0:T(8,128)S(1)}, u32[]{:S(2)}) copy-start(f32[896,128]{1,0:T(8,128)S(1)} %get-tuple-element.86.own0) | copy-start | bytes 1376260
  134.8 1.9 collective-permute-start.29
  134.9 2.5 %collective-permute-start.28 = (f32[896,128]{1,0:T(8,128)S(1)}, f32[896,128]{1,0:T(8,128)S(1)}, u32[]{:S(2)}, u32[]{:S(2)}) collective-permute-start(f32[896,128]{1,0:T(8,128)S(1)} %get-tuple-element.86.own0), channel_id=1, source_target_pairs={{0,4},{4,0},{8,12},{12,8},{1,5},{5,1},{9,13},{13,9},{2,6},{6,2},{1... | collective-permute-start | bytes 1376264 | tf_op jit(solution)/shard_map/ppermute | solution.py:430
  135.8 2.2 %copy-start.5 = (f32[832,128]{1,0:T(8,128)}, f32[832,128]{1,0:T(8,128)S(1)}, u32[]{:S(2)}) copy-start(f32[832,128]{1,0:T(8,128)S(1)} %bitcast_select_fusion.2.own2) | copy-start | bytes 1277956
  135.8 2.2 %collective-permute-start.30 = (f32[832,128]{1,0:T(8,128)S(1)}, f32[832,128]{1,0:T(8,128)S(1)}, u32[]{:S(2)}, u32[]{:S(2)}) collective-permute-start(f32[832,128]{1,0:T(8,128)S(1)} %bitcast_select_fusion.2.own2), channel_id=1, source_target_pairs={{0,4},{4,0},{8,12},{12,8},{1,5},{5,1},{9,13},{13,9},{2,6},{6,2},{1... | collective-permute-start | bytes 1277960 | tf_op jit(solution)/shard_map/ppermute | solution.py:430
  136.7 1.3 copy-start.19
  137.4 0.8 copy-start.20
  138.2 0.8 copy-start.21
  185.9 8.3 %collective-permute-start.35 = (f32[424,128]{1,0:T(8,128)S(1)}, f32[424,128]{1,0:T(8,128)S(1)}, u32[]{:S(2)}, u32[]{:S(2)}) collective-permute-start(f32[424,128]{1,0:T(8,128)S(1)} %get-tuple-element.83), channel_id=1, source_target_pairs={{0,16},{16,0},{1,17},{17,1},{2,18},{18,2},{3,19},{19,3},{4,20},{20... | collective-permute-start | bytes 651272 | tf_op jit(solution)/shard_map/ppermute | solution.py:430
  186.5 8.2 %collective-permute-start.34 = (f32[424,128]{1,0:T(8,128)S(1)}, f32[424,128]{1,0:T(8,128)S(1)}, u32[]{:S(2)}, u32[]{:S(2)}) collective-permute-start(f32[424,128]{1,0:T(8,128)S(1)} %get-tuple-element.83), channel_id=1, source_target_pairs={{0,1},{1,0},{2,3},{3,2},{4,5},{5,4},{6,7},{7,6},{8,9},{9,8},{10,11... | collective-permute-start | bytes 651272 | tf_op jit(solution)/shard_map/ppermute | solution.py:430
  186.5 12.3 %collective-permute-start.32 = (f32[424,128]{1,0:T(8,128)S(1)}, f32[424,128]{1,0:T(8,128)S(1)}, u32[]{:S(2)}, u32[]{:S(2)}) collective-permute-start(f32[424,128]{1,0:T(8,128)S(1)} %get-tuple-element.84), channel_id=1, source_target_pairs={{0,16},{16,0},{1,17},{17,1},{2,18},{18,2},{3,19},{19,3},{4,20},{20... | collective-permute-start | bytes 651272 | tf_op jit(solution)/shard_map/ppermute | solution.py:430
  188.0 10.8 %collective-permute-start.31 = (f32[424,128]{1,0:T(8,128)S(1)}, f32[424,128]{1,0:T(8,128)S(1)}, u32[]{:S(2)}, u32[]{:S(2)}) collective-permute-start(f32[424,128]{1,0:T(8,128)S(1)} %get-tuple-element.84), channel_id=1, source_target_pairs={{0,1},{1,0},{2,3},{3,2},{4,5},{5,4},{6,7},{7,6},{8,9},{9,8},{10,11... | collective-permute-start | bytes 651272 | tf_op jit(solution)/shard_map/ppermute | solution.py:430
  194.2 12.0 %copy-start.6 = (f32[424,128]{1,0:T(8,128)}, f32[424,128]{1,0:T(8,128)S(1)}, u32[]{:S(2)}) copy-start(f32[424,128]{1,0:T(8,128)S(1)} %collective-permute-done.35.refs_4_) | copy-start | bytes 651268
  194.2 5.2 %collective-permute-start.41 = (f32[424,128]{1,0:T(8,128)S(1)}, f32[424,128]{1,0:T(8,128)S(1)}, u32[]{:S(2)}, u32[]{:S(2)}) collective-permute-start(f32[424,128]{1,0:T(8,128)S(1)} %collective-permute-done.35.refs_4_), channel_id=1, source_target_pairs={{0,4},{4,0},{8,12},{12,8},{1,5},{5,1},{9,13},{13,9},{2,6},{6,2},{1... | collective-permute-start | bytes 651272 | tf_op jit(solution)/shard_map/ppermute | solution.py:430
  194.7 11.5 %copy-start.7 = (f32[424,128]{1,0:T(8,128)}, f32[424,128]{1,0:T(8,128)S(1)}, u32[]{:S(2)}) copy-start(f32[424,128]{1,0:T(8,128)S(1)} %collective-permute-done.34.refs_3_) | copy-start | bytes 651268
  194.7 8.0 %collective-permute-start.36 = (f32[424,128]{1,0:T(8,128)S(1)}, f32[424,128]{1,0:T(8,128)S(1)}, u32[]{:S(2)}, u32[]{:S(2)}) collective-permute-start(f32[424,128]{1,0:T(8,128)S(1)} %collective-permute-done.34.refs_3_), channel_id=1, source_target_pairs={{0,16},{16,0},{1,17},{17,1},{2,18},{18,2},{3,19},{19,3},{4,20},{20... | collective-permute-start | bytes 651272 | tf_op jit(solution)/shard_map/ppermute | solution.py:430
  198.8 7.4 %copy-start.8 = (f32[424,128]{1,0:T(8,128)}, f32[424,128]{1,0:T(8,128)S(1)}, u32[]{:S(2)}) copy-start(f32[424,128]{1,0:T(8,128)S(1)} %collective-permute-done.32.refs_1_) | copy-start | bytes 651268
  198.8 5.9 %collective-permute-start.33 = (f32[424,128]{1,0:T(8,128)S(1)}, f32[424,128]{1,0:T(8,128)S(1)}, u32[]{:S(2)}, u32[]{:S(2)}) collective-permute-start(f32[424,128]{1,0:T(8,128)S(1)} %collective-permute-done.32.refs_1_), channel_id=1, source_target_pairs={{0,1},{1,0},{2,3},{3,2},{4,5},{5,4},{6,7},{7,6},{8,9},{9,8},{10,11... | collective-permute-start | bytes 651272 | tf_op jit(solution)/shard_map/ppermute | solution.py:430
  198.8 5.9 %collective-permute-start.40 = (f32[424,128]{1,0:T(8,128)S(1)}, f32[424,128]{1,0:T(8,128)S(1)}, u32[]{:S(2)}, u32[]{:S(2)}) collective-permute-start(f32[424,128]{1,0:T(8,128)S(1)} %collective-permute-done.34.refs_3_), channel_id=1, source_target_pairs={{0,4},{4,0},{8,12},{12,8},{1,5},{5,1},{9,13},{13,9},{2,6},{6,2},{1... | collective-permute-start | bytes 651272 | tf_op jit(solution)/shard_map/ppermute | solution.py:430
  198.8 7.4 %copy-start.9 = (f32[424,128]{1,0:T(8,128)}, f32[424,128]{1,0:T(8,128)S(1)}, u32[]{:S(2)}) copy-start(f32[424,128]{1,0:T(8,128)S(1)} %collective-permute-done.31.refs_0_) | copy-start | bytes 651268
  198.8 5.9 %collective-permute-start.38 = (f32[424,128]{1,0:T(8,128)S(1)}, f32[424,128]{1,0:T(8,128)S(1)}, u32[]{:S(2)}, u32[]{:S(2)}) collective-permute-start(f32[424,128]{1,0:T(8,128)S(1)} %collective-permute-done.32.refs_1_), channel_id=1, source_target_pairs={{0,4},{4,0},{8,12},{12,8},{1,5},{5,1},{9,13},{13,9},{2,6},{6,2},{1... | collective-permute-start | bytes 651272 | tf_op jit(solution)/shard_map/ppermute | solution.py:430
  199.3 6.9 %copy-start.10 = (f32[424,128]{1,0:T(8,128)}, f32[424,128]{1,0:T(8,128)S(1)}, u32[]{:S(2)}) copy-start(f32[424,128]{1,0:T(8,128)S(1)} %collective-permute-done.41.refs_10_) | copy-start | bytes 651268
  199.3 5.4 %collective-permute-start.37 = (f32[424,128]{1,0:T(8,128)S(1)}, f32[424,128]{1,0:T(8,128)S(1)}, u32[]{:S(2)}, u32[]{:S(2)}) collective-permute-start(f32[424,128]{1,0:T(8,128)S(1)} %collective-permute-done.31.refs_0_), channel_id=1, source_target_pairs={{0,4},{4,0},{8,12},{12,8},{1,5},{5,1},{9,13},{13,9},{2,6},{6,2},{1... | collective-permute-start | bytes 651272 | tf_op jit(solution)/shard_map/ppermute | solution.py:430
  202.7 3.5 %copy-start.11 = (f32[424,128]{1,0:T(8,128)}, f32[424,128]{1,0:T(8,128)S(1)}, u32[]{:S(2)}) copy-start(f32[424,128]{1,0:T(8,128)S(1)} %collective-permute-done.36.refs_5_) | copy-start | bytes 651268
  202.7 2.1 collective-permute-start.42
  204.7 1.5 copy-start.12
  204.7 1.5 collective-permute-start.39
  204.7 1.5 copy-start.13
  204.7 1.5 copy-start.14
  204.8 1.5 copy-start.15
  204.8 1.5 copy-start.16
  (1 other events, 0.7 us)
